TPU v7x, 512 devices: a whole 4x8x8 slice. The times are simulated.
512 devices in a mesh: wave: 64 (over z, y), lev: 8 (over x, core).
Axes of the slice: x: 4, y: 8, z: 8, core: 2. Of those that a mesh axis runs over, the one named last changes fastest.
Arguments:
- control: bfloat16 [2, 256, 256, 2, 512], P(None, 'wave', 'lev'), may hold values from -6 to 6
- wave_of_slot: int32 [256], replicated, may hold values from 0 to 255, each once
- legendre: bfloat16 [256, 256, 256], P('wave', 'lev'), may hold values from -0.375 to 0.375
- vertical: bfloat16 [4, 4, 128, 128], replicated, may hold values from -0.5 to 0.5
- points: int32 [256], P('wave'), may hold values from 128 to 512
- lat_band: int32 [256], P('wave'), may hold values from 0 to 7, never falling along the last dimension, each value on 1 to 64 neighbouring positions
- grid_scale: float32 [8, 512], P(None, 'lev'), may hold values from 0.5 to 2
- obs_weight: bfloat16 [256, 512, 512], P('wave', 'lev'), may hold values from 0.19921875 to 1
Outputs:
- increment: bfloat16 [2, 256, 512, 512], P(None, 'wave', 'lev')
- gradient: bfloat16 [2, 256, 256, 2, 512], P(None, 'wave', 'lev')
Inputs may be any that keep to these rules, and one draw needn't show every extreme that they name: `wave_of_slot`: each zonal wavenumber 0 to 255 stands in exactly one slot. `lat_band`: band numbers never fall from one latitude to the next, and each band covers 1 to 64 latitudes.
All inputs are finite; a program needn't handle non-finite values.
Results may differ from a plain program's by a relative error of at most 0.007.
Values may be sent and summed in bfloat16 or wider, within the bound.
A program may use at most 64 MiB of HBM per device.

v0:
```python
import math

import jax
import jax.numpy as jnp
from jax import lax
from jax.sharding import PartitionSpec as P

WAVES = 256
LONGITUDES = 512
LEVELS = 128
VARIABLES = 4
COV_BANDS = 4


def in_order(tiles, dim):
    lengths = list(tiles.shape[1:])
    lengths[dim] *= tiles.shape[0]
    return jnp.moveaxis(tiles, 0, dim).reshape(lengths)


def sent_to_all(array, axis):
    devices = lax.axis_size(axis)
    return lax.all_to_all(
        jnp.broadcast_to(array[None], (devices, *array.shape)), axis, 0, 0, tiled=True
    )


def collect(array, axis, dim):
    return in_order(sent_to_all(array, axis), dim)


def fourier_table(wave_ids, lat_points):
    lon_index = jnp.arange(LONGITUDES, dtype=jnp.int32)
    remainder = wave_ids[None, :, None] * lon_index[None, None, :] % lat_points[:, None, None]
    angles = (
        2.0
        * math.pi
        * remainder.astype(jnp.float32)
        / lat_points.astype(jnp.float32)[:, None, None]
    )
    factor = jnp.where(wave_ids == 0, 1.0, 2.0).astype(jnp.float32) / math.sqrt(4.0 * WAVES)
    inside = lon_index[None, None, :] < lat_points[:, None, None]
    cosine = jnp.where(inside, factor[None, :, None] * jnp.cos(angles), 0.0)
    sine = jnp.where(inside, -factor[None, :, None] * jnp.sin(angles), 0.0)
    return jnp.stack([cosine, sine], axis=2).astype(jnp.bfloat16)


def vertical_apply(field, vertical, live_rows, band_of, forward):
    members, slots, rows_dev = (field.shape[0], field.shape[1], field.shape[2])
    shaped = field.reshape(members, slots, rows_dev, 2, VARIABLES, LEVELS)
    form = "eskpam,alm->eskpal" if forward else "eskpal,alm->eskpam"
    summed = jnp.zeros(shaped.shape, jnp.float32)
    for index_band in range(COV_BANDS):
        partial_value = jnp.einsum(
            form, shaped, vertical[index_band], preferred_element_type=jnp.float32
        )
        chosen = live_rows & (band_of == index_band)
        summed = summed + jnp.where(chosen[None, :, :, None, None, None], partial_value, 0.0)
    return summed.reshape(field.shape).astype(jnp.bfloat16)


def to_bands(values):
    return lax.all_to_all(values, "wave", split_axis=2, concat_axis=1, tiled=True)


def shards(control, wave_of_slot, legendre, vertical, points, lat_band, grid_scale, obs_weight):
    members, slots, rows_dev = (control.shape[0], control.shape[1], control.shape[2])
    slot_start = lax.axis_index("wave") * slots
    row_start = lax.axis_index("lev") * rows_dev
    own_waves = lax.dynamic_slice_in_dim(wave_of_slot, slot_start, slots)
    row_index = row_start + jnp.arange(rows_dev, dtype=jnp.int32)
    totals_n = own_waves[:, None] + row_index[None, :]
    live_rows = totals_n <= WAVES - 1
    band_of = jnp.minimum(totals_n * COV_BANDS // WAVES, COV_BANDS - 1)
    spectral = vertical_apply(control, vertical, live_rows, band_of, True)
    columns = lax.all_to_all(spectral, "lev", split_axis=4, concat_axis=2, tiled=True)
    col_dev = columns.shape[4]
    width = 2 * col_dev
    all_rows = columns.shape[2]
    columns = columns.reshape(members, slots, all_rows, width)
    coeffs = jnp.einsum(
        "skt,eskq->estq", collect(legendre, "lev", 1), columns, preferred_element_type=jnp.float32
    )
    coeffs = coeffs.astype(jnp.bfloat16)
    by_lat = to_bands(coeffs)
    wave_count = by_lat.shape[1]
    lat_dev = by_lat.shape[2]
    by_lat = by_lat.reshape(members, wave_count, lat_dev, 2, col_dev)
    fourier = fourier_table(wave_of_slot, points)
    synthesis = jnp.einsum("tspj,estpc->etcj", fourier, by_lat, preferred_element_type=jnp.float32)
    chooser = (
        lat_band[:, None] == jnp.arange(grid_scale.shape[0], dtype=jnp.int32)[None, :]
    ).astype(jnp.float32)
    lat_scale = jnp.dot(chooser, grid_scale, precision=lax.Precision.HIGHEST)
    increment = (synthesis * lat_scale[None, :, :, None]).astype(jnp.bfloat16)
    weighted = (
        increment.astype(jnp.float32) * obs_weight.astype(jnp.float32) * lat_scale[None, :, :, None]
    ).astype(jnp.bfloat16)
    adjoint_fourier = jnp.einsum(
        "tspj,etcj->etspc", fourier, weighted, preferred_element_type=jnp.float32
    )
    adjoint_fourier = adjoint_fourier.astype(jnp.bfloat16).reshape(
        members, lat_dev, wave_count, width
    )
    band_rows = to_bands(adjoint_fourier)
    adjoint_coeffs = jnp.einsum(
        "skt,etsq->eskq", collect(legendre, "lev", 1), band_rows, preferred_element_type=jnp.float32
    )
    adjoint_coeffs = adjoint_coeffs.astype(jnp.bfloat16).reshape(
        members, slots, all_rows, 2, col_dev
    )
    rows_back = lax.all_to_all(adjoint_coeffs, "lev", split_axis=2, concat_axis=4, tiled=True)
    gradient = vertical_apply(rows_back, vertical, live_rows, band_of, False)
    return (increment, gradient)


def solution(mesh):
    in_specs = (
        P(None, "wave", "lev", None, None),
        P(),
        P("wave", "lev", None),
        P(),
        P("wave"),
        P("wave"),
        P(None, "lev"),
        P("wave", "lev", None),
    )
    out_specs = (P(None, "wave", "lev", None), P(None, "wave", "lev", None, None))
    return jax.shard_map(shards, mesh=mesh, in_specs=in_specs, out_specs=out_specs, check_vma=False)
```

profile of v0, /device:TPU:1, one launch (start us, length us, event | category | flops | bytes accessed | tf_op | source)
XLA Modules:
  0.0 145.6 jit_solution(16223339216924004646)
XLA Ops:
  0.6 0.0 copy-start
  0.6 0.0 copy-start.1
  0.7 1.4 reshape.278
  2.1 0.8 dynamic_slice.3
  2.9 0.1 compare_and_fusion.3
  3.0 1.2 convolution_select_fusion.4
  4.2 0.3 convolution_select_fusion.5
  4.5 0.3 convolution_select_fusion.6
  4.8 0.4 fusion.19
  5.2 1.8 %copy.77 = bf16[2,4,32,2,4,128]{2,3,1,0,5,4:T(2,128)(2,1)S(1)} copy(bf16[2,4,32,2,4,128]{5,2,3,1,0,4:T(8,128)(2,1)S(1)} %fusion.19) | data formatting | bytes 1048576 | tf_op jit(solution)/shard_map/convert_element_type | solution.py:59
  7.0 0.0 copy-start.8
  7.0 0.0 copy-start.10
  7.0 0.0 copy-start.9
  7.0 2.0 %reshape.295 = bf16[8,2,16384]{2,1,0:T(2,128)(2,1)S(1)} reshape(bf16[512,2,4,2,32]{4,3,2,1,0:T(2,128)(2,1)S(1)} %bitcast.107) | data formatting | bytes 1048576
  9.1 18.6 %all_to_all.69 = bf16[8,2,16384]{2,1,0:T(2,128)(2,1)S(1)} all-to-all(bf16[8,2,16384]{2,1,0:T(2,128)(2,1)S(1)} %reshape.295), channel_id=1, replica_groups=mesh['wave'=64,'lev'=8] {'lev'}, dimensions={0} | all-to-all | bytes 1048576 | tf_op jit(solution)/shard_map/all_to_all | solution.py:76
  27.6 0.9 broadcast_in_dim.118
  28.5 5.1 %all-to-all-start.1 = ((bf16[8,4,32,256]{3,2,1,0:T(8,128)(2,1)}), bf16[8,4,32,256]{3,2,1,0:T(8,128)(2,1)}, u32[]{:S(2)}, u32[]{:S(2)}) async-start(bf16[8,4,32,256]{3,2,1,0:T(8,128)(2,1)} %broadcast_in_dim.118), calls=%async_computation.1 | async-start | bytes 1048576 | tf_op jit(solution)/shard_map/all_to_all | solution.py:23
  33.6 0.1 iota_compare_fusion
  33.7 1.1 reshape.296
  34.7 3.0 %copy.78 = bf16[2,4,32,2,8,64]{5,4,2,3,1,0:T(8,128)(2,1)S(1)} copy(bf16[2,4,32,2,8,64]{2,3,1,0,5,4:T(2,128)(2,1)S(1)} %bitcast.108) | data formatting | bytes 1048576 | tf_op jit(solution)/shard_map/all_to_all | solution.py:76
  37.7 1.1 copy.83
  38.8 0.5 reshape.294
  39.3 3.8 %all-to-all-done.1 = bf16[8,4,32,256]{3,2,1,0:T(8,128)(2,1)} async-done(((bf16[8,4,32,256]{3,2,1,0:T(8,128)(2,1)}), bf16[8,4,32,256]{3,2,1,0:T(8,128)(2,1)}, u32[]{:S(2)}, u32[]{:S(2)}) %all-to-all-start.1) | async-done | bytes 524320 | tf_op jit(solution)/shard_map/all_to_all | solution.py:23
  43.0 1.1 copy.47
  44.1 0.0 copy-start.7
  44.1 0.0 copy-start.11
  44.2 0.4 fusion.18
  44.5 1.2 copy.49
  45.7 12.8 %all-to-all-start.2 = ((bf16[2,4,256,128]{3,0,1,2:T(2,128)(2,1)}), bf16[2,4,256,128]{3,0,1,2:T(2,128)(2,1)S(1)}, u32[]{:S(2)}, u32[]{:S(2)}) async-start(bf16[2,4,256,128]{3,0,1,2:T(2,128)(2,1)} %copy.49), calls=%async_computation.2 | async-start | bytes 1048576 | tf_op jit(solution)/shard_map/all_to_all | solution.py:63
  58.5 0.9 convert_element_type.68
  59.4 0.2 fusion.57
  59.6 0.1 iota_multiply_fusion
  59.7 28.9 %select_convert_fusion.1 = (bf16[4,256,1,512]{3,1,2,0:T(8,128)(2,1)S(1)}, bf16[4,256,1,512]{3,1,2,0:T(8,128)(2,1)}) fusion(f32[256]{0:T(256)S(1)} %get-tuple-element.14, f32[4]{0:T(128)S(1)} %get-tuple-element.17, pred[4]{0:T(512)(128)(4,1)S(1)} %broadcast_compare_fusion, s32[4]{0:T(128)S(1)} %get-tuple-element.16, s32[256,512]{1,0:T(8,128)S(1)} %iota_multiply_fusion, ...), kind=kLoop, calls=%fused_computation.9 | loop fusion | flops 8388608 | bytes 2625572 | tf_op jit(solution)/shard_map/convert.1
  88.6 0.0 all-to-all-done.2
  88.7 0.1 copy.50
  88.7 0.2 copy.51
  88.9 0.4 reshape.281
  89.3 0.0 copy-start.4
  89.4 2.0 %fusion.17 = bf16[2,4,64,512]{3,2,0,1:T(8,128)(2,1)S(1)} fusion(bf16[4,256,1,512]{3,1,2,0:T(8,128)(2,1)} %get-tuple-element.9, bf16[4,256,1,512]{3,1,2,0:T(8,128)(2,1)S(1)} %get-tuple-element.8, bf16[2,256,4,2,64]{4,3,2,1,0:T(2,128)(2,1)S(1)} %reshape.281, f32[4,64]{1,0:T(4,128)S(1)} %fusion.57), kind=kOutput, calls=%fused_computation.35 | convolution fusion | flops 270008320 | bytes 3146752 | tf_op jit(solution)/shard_map/tspj,estpc->etcj/dot_general | solution.py:90
  91.3 0.0 copy-start.5
  91.4 0.8 fusion.15
  92.2 0.3 copy.53
  92.5 27.8 %all_to_all.70 = bf16[2,4,256,128]{3,1,0,2:T(4,128)(2,1)S(1)} all-to-all(bf16[2,4,256,128]{3,1,0,2:T(4,128)(2,1)S(1)} %copy.53), channel_id=1, replica_groups=mesh['wave'=64,'lev'=8] {'wave'}, dimensions={2} | all-to-all | bytes 1048576 | tf_op jit(solution)/shard_map/all_to_all | solution.py:63
  120.3 0.1 copy.54
  120.4 0.4 copy.55
  120.8 0.3 convolution_convert_fusion
  121.2 0.0 copy-start.6
  121.2 1.0 copy.57
  122.2 1.5 %reshape.297 = bf16[8,2,16384]{2,1,0:T(2,128)(2,1)} reshape(bf16[256,2,4,2,64]{4,3,2,1,0:T(2,128)(2,1)S(1)} %bitcast.112) | data formatting | bytes 1048576
  123.7 7.9 %all-to-all-start.4 = ((bf16[8,2,16384]{2,1,0:T(2,128)(2,1)}), bf16[8,2,16384]{2,1,0:T(2,128)(2,1)S(1)}, u32[]{:S(2)}, u32[]{:S(2)}) async-start(bf16[8,2,16384]{2,1,0:T(2,128)(2,1)} %reshape.297), calls=%async_computation.4 | async-start | bytes 1048576 | tf_op jit(solution)/shard_map/all_to_all | solution.py:112
  131.6 0.8 copy.65
  132.4 8.5 %all-to-all-done.4 = bf16[8,2,16384]{2,1,0:T(2,128)(2,1)S(1)} async-done(((bf16[8,2,16384]{2,1,0:T(2,128)(2,1)}), bf16[8,2,16384]{2,1,0:T(2,128)(2,1)S(1)}, u32[]{:S(2)}, u32[]{:S(2)}) %all-to-all-start.4) | async-done | bytes 524320 | tf_op jit(solution)/shard_map/all_to_all | solution.py:112
  141.0 0.7 reshape.298
  141.7 0.3 copy.58
  141.9 0.0 copy-start.2
  141.9 0.4 copy.59
  142.4 0.5 reshape.284
  142.8 0.1 copy-done.2
  143.0 0.3 convolution_select_fusion.1
  143.3 0.3 convolution_select_fusion.2
  143.5 0.3 convolution_select_fusion
  143.8 0.3 fusion.20
  144.2 0.4 copy.81
  144.6 1.0 reshape.293
  (16 shorter events, 0.0 us)
Async XLA Ops:
  0.6 58.8 %copy-start = (f32[8,64]{1,0:T(8,128)S(1)}, f32[8,64]{1,0:T(8,128)}, u32[]{:S(2)}) copy-start(f32[8,64]{1,0:T(8,128)} %param.14) | copy-start | bytes 6148
  0.6 3.5 %copy-start.1 = (bf16[4,4,128,128]{3,2,1,0:T(8,128)(2,1)S(1)}, bf16[4,4,128,128]{3,2,1,0:T(8,128)(2,1)}, u32[]{:S(2)}) copy-start(bf16[4,4,128,128]{3,2,1,0:T(8,128)(2,1)} %param.11) | copy-start | bytes 1572868
  7.0 20.6 %copy-start.8 = (bf16[4,32,256]{2,1,0:T(8,128)(2,1)S(1)}, bf16[4,32,256]{2,1,0:T(8,128)(2,1)}, u32[]{:S(2)}) copy-start(bf16[4,32,256]{2,1,0:T(8,128)(2,1)} %param.10) | copy-start | bytes 196612
  7.0 26.5 %copy-start.10 = (s32[4]{0:T(128)S(1)}, s32[4]{0:T(128)}, u32[]{:S(2)}) copy-start(s32[4]{0:T(128)} %param.12) | copy-start | bytes 52
  7.0 26.6 %copy-start.9 = (s32[256]{0:T(256)S(1)}, s32[256]{0:T(256)}, u32[]{:S(2)}) copy-start(s32[256]{0:T(256)} %param.9) | copy-start | bytes 3076
  28.5 14.5 %all-to-all-start.1 = ((bf16[8,4,32,256]{3,2,1,0:T(8,128)(2,1)}), bf16[8,4,32,256]{3,2,1,0:T(8,128)(2,1)}, u32[]{:S(2)}, u32[]{:S(2)}) async-start(bf16[8,4,32,256]{3,2,1,0:T(8,128)(2,1)} %broadcast_in_dim.118), calls=%async_computation.1 | async-start | bytes 1048576 | tf_op jit(solution)/shard_map/all_to_all | solution.py:23
  44.1 14.4 %copy-start.7 = (bf16[4,64,512]{2,1,0:T(8,128)(2,1)S(1)}, bf16[4,64,512]{2,1,0:T(8,128)(2,1)}, u32[]{:S(2)}) copy-start(bf16[4,64,512]{2,1,0:T(8,128)(2,1)} %param.15) | copy-start | bytes 786436
  44.1 15.3 %copy-start.11 = (s32[4]{0:T(128)S(1)}, s32[4]{0:T(128)}, u32[]{:S(2)}) copy-start(s32[4]{0:T(128)} %param.13) | copy-start | bytes 52
  45.7 43.0 %all-to-all-start.2 = ((bf16[2,4,256,128]{3,0,1,2:T(2,128)(2,1)}), bf16[2,4,256,128]{3,0,1,2:T(2,128)(2,1)S(1)}, u32[]{:S(2)}, u32[]{:S(2)}) async-start(bf16[2,4,256,128]{3,0,1,2:T(2,128)(2,1)} %copy.49), calls=%async_computation.2 | async-start | bytes 1048576 | tf_op jit(solution)/shard_map/all_to_all | solution.py:63
  89.3 2.0 %copy-start.3 = (bf16[4,256,1,512]{3,1,2,0:T(8,128)(2,1)S(1)}, bf16[4,256,1,512]{3,1,2,0:T(8,128)(2,1)}, u32[]{:S(2)}) copy-start(bf16[4,256,1,512]{3,1,2,0:T(8,128)(2,1)} %get-tuple-element.9) | copy-start | bytes 3145732
  89.3 2.0 %copy-start.4 = (f32[4,64,512]{2,1,0:T(8,128)S(1)}, f32[4,64,512]{2,1,0:T(8,128)}, u32[]{:S(2)}) copy-start(f32[4,64,512]{2,1,0:T(8,128)} %convert_element_type.68) | copy-start | bytes 1572868
  91.3 0.9 copy-start.5
  121.2 10.4 %copy-start.6 = (bf16[2,4,64,512]{3,2,0,1:T(8,128)(2,1)S(1)}, bf16[2,4,64,512]{3,2,0,1:T(8,128)(2,1)}, u32[]{:S(2)}) copy-start(bf16[2,4,64,512]{3,2,0,1:T(8,128)(2,1)} %copy-done.5) | copy-start | bytes 1572868
  123.7 17.3 %all-to-all-start.4 = ((bf16[8,2,16384]{2,1,0:T(2,128)(2,1)}), bf16[8,2,16384]{2,1,0:T(2,128)(2,1)S(1)}, u32[]{:S(2)}, u32[]{:S(2)}) async-start(bf16[8,2,16384]{2,1,0:T(2,128)(2,1)} %reshape.297), calls=%async_computation.4 | async-start | bytes 1048576 | tf_op jit(solution)/shard_map/all_to_all | solution.py:112
  141.9 1.0 copy-start.2
where the time goes:
time: 146 us
  blocking collectives  46.3 us (32%)
  other arithmetic  30.1 us (21%)
  starting transfers between devices  25.8 us (18%)
  local copies, waits for them, and re-layouts  23 us (16%)
  waiting for transfers between devices  12.3 us (8%)
  matrix products  7.04 us (5%)
    another operation x1, other arithmetic  28.9 us
    all_to_all x1, blocking collectives, to_bands(): lax.all_to_all(values, 'wave', split_axis=2, concat_axis=1, tiled=True)  27.8 us
    all_to_all x1, blocking collectives, shards(): lax.all_to_all(spectral, 'lev', split_axis=4, concat_axis=2, tiled=True)  18.6 us
    all_to_all x1, starting transfers between devices, to_bands(): lax.all_to_all(values, 'wave', split_axis=2, concat_axis=1, tiled=True)  12.8 us
    all_to_all x1, waiting for transfers between devices, shards(): lax.all_to_all(adjoint_coeffs, 'lev', split_axis=2, concat_axis=4, tiled=...  8.55 us
    all_to_all x1, starting transfers between devices, shards(): lax.all_to_all(adjoint_coeffs, 'lev', split_axis=2, concat_axis=4, tiled=...  7.88 us
    unnamed x31, local copies, waits for them, and re-layouts  7.72 us
    all_to_all x1, starting transfers between devices, sent_to_all(): lax.all_to_all(jnp.broadcast_to(array[None], (devices, *array.shape)), ax...  5.06 us
  transfers between devices with their start and end apart: 3, of which 2 were waited for; matrix products, arithmetic and copies ran while one was open for 25% of the time, Pallas kernels for 0%

commit v1 on v0

v1 whole, which is shorter than its diff:
```python
import functools

import jax
import jax.numpy as jnp
from jax import lax
from jax.experimental import pallas as pl
from jax.experimental.pallas import tpu as pltpu
from jax.sharding import PartitionSpec as P

WAVES = 256
LONGITUDES = 512
COV_BANDS = 4
VARIABLES = 4
MESH = pl.DeviceIdType.MESH
F32 = jnp.float32
BF16 = jnp.bfloat16
FAR_FIRST = (4, 3, 5, 2, 6, 1, 7)
SIN = (6.283185302498671, -41.34170040100665, 81.6051311559332, -76.70301094142194,
       42.02588917305049, -14.899698808670236, 3.237922486217859)
COS = (0.9999999998851921, -19.739208743292323, 64.93938906426658, -85.45665800487392,
       60.24212744331612, -26.404643265364264, 7.800052913395129, -1.453015691570865)


def polynomial(terms, s):
    value = jnp.full(s.shape, terms[-1], F32)
    for term in terms[-2::-1]:
        value = value * s + term
    return value


def dot(a, b, dims=((1,), (0,))):
    return lax.dot_general(a, b, (dims, ((), ())), preferred_element_type=F32)


def kernel(
    waves_s, points_s, band_s, waves_v, ctl_h, leg_h, ver_h, scale_h, obs_h,
    inc_h, grad_h,
    ctl, ver, own_leg, scale, obs, inc, grad,
    mask, mix, send_f, recv_f, leg, leg_t, wcol, table,
    a1, b1y, b1z, c1, xf, a2, b2y, b2z, c2, send_b, recv_b,
    in_sem, out_sem, leg_ss, leg_rs, lev_ss, lev_rs, wave_ss, wave_rs,
):
    wave = lax.axis_index("wave")
    lev = lax.axis_index("lev")
    z = wave // 8
    y = lax.rem(wave, 8)

    ins = [
        pltpu.make_async_copy(src, dst, in_sem.at[i])
        for i, (src, dst) in enumerate(
            ((ctl_h, ctl), (ver_h, ver), (leg_h, own_leg), (scale_h, scale), (obs_h, obs))
        )
    ]
    for copy in ins:
        copy.start()

    barrier = pltpu.get_barrier_semaphore()

    def along(i):
        return (
            (wave, lax.rem(lev + i, 8)),
            (z * 8 + lax.rem(y + i, 8), lev),
            (lax.rem(z + i, 8) * 8 + y, lev),
        )

    for i in FAR_FIRST:
        for who in along(i):
            pl.semaphore_signal(barrier, inc=1, device_id=who, device_id_type=MESH)

    row = lax.broadcasted_iota(jnp.int32, (128, 128), 0)
    slot = row // 32
    total = lev * 32 + lax.rem(row, 32)
    for s in range(4):
        total = total + jnp.where(slot == s, waves_s[wave * 4 + s], 0)
    band = jnp.minimum(total * COV_BANDS // WAVES, COV_BANDS - 1)
    for b in range(COV_BANDS):
        chosen = (total <= WAVES - 1) & (band == b)
        mask[b] = jnp.where(chosen, 1.0, 0.0).astype(BF16)

    ins[1].wait()

    def lay(i, carry):
        zero = jnp.zeros((64, 128), BF16)
        v = ver[i]
        for half in range(2):
            piece = v[half * 64 : half * 64 + 64]
            mix[i, half * 128 : half * 128 + 64, 0:128] = piece
            mix[i, half * 128 : half * 128 + 64, 128:256] = zero
            mix[i, half * 128 + 64 : half * 128 + 128, 0:128] = zero
            mix[i, half * 128 + 64 : half * 128 + 128, 128:256] = piece
        return carry

    lax.fori_loop(0, COV_BANDS * VARIABLES, lay, 0)

    ins[0].wait()
    for a in range(VARIABLES):
        both = [ctl[:, a * 128 : a * 128 + 128], ctl[:, 512 + a * 128 : 640 + a * 128]]
        out = jnp.zeros((256, 256), F32)
        for b in range(COV_BANDS):
            m = jnp.concatenate([mask[b], mask[b]], axis=0)
            x = jnp.concatenate([part * m for part in both], axis=1)
            out = out + dot(x, mix[b * VARIABLES + a], ((1,), (1,)))
        out = out.astype(BF16)
        for half in range(2):
            send_f[2 * a + half] = out[:, half * 128 : half * 128 + 128].reshape(2, 4, 32, 128)

    place = lax.broadcasted_iota(jnp.int32, (256, 128), 0)
    wanted = lax.rem(place, 128) // 2 * 4 + place // 128 * 2 + lax.rem(place, 2)
    lane = lax.broadcasted_iota(jnp.int32, (256, 128), 1)
    found = jnp.zeros((256, 128), F32)
    for i in range(2):
        numbers = waves_v[i : i + 1, :].astype(F32)
        found = found + jnp.where(wanted == lane + i * 128, numbers, 0.0)
    wcol[...] = jnp.broadcast_to(jnp.sum(found, axis=1, keepdims=True), (256, 128))

    for t in range(4):
        count = jnp.full((16, LONGITUDES), points_s[t], jnp.int32).astype(F32)
        inverse = 1.0 / count

        def rows_of_table(i, carry, t=t, count=count, inverse=inverse):
            at = pl.multiple_of(i * 16, 16)
            w = wcol[pl.ds(at, 16), :]
            w = jnp.concatenate([w, w, w, w], axis=1)
            j = lax.broadcasted_iota(jnp.int32, (16, LONGITUDES), 1).astype(F32)
            product = w * j
            turns = jnp.floor(product * inverse + 0.5)
            x = (product - turns * count) * inverse
            s = x * x
            factor = jnp.where(w == 0.0, 1.0, 2.0) * (1.0 / 32.0)
            factor = jnp.where(j < count, factor, 0.0)
            table[t, 0, pl.ds(at, 16), :] = (factor * polynomial(COS, s)).astype(BF16)
            table[t, 1, pl.ds(at, 16), :] = (-factor * (x * polynomial(SIN, s))).astype(BF16)
            return carry

        lax.fori_loop(0, 16, rows_of_table, 0)

    ins[2].wait()
    pl.semaphore_wait(barrier, 21)

    def lev_peer(i):
        return lax.rem(lev + i, 8)

    def remote(src, dst, ss, rs, who):
        pltpu.make_async_remote_copy(
            src, dst, ss, rs, device_id=who, device_id_type=MESH
        ).start()

    def arrived(buffer, sem):
        pltpu.make_async_copy(buffer, buffer, sem).wait()

    def send_leg(h):
        for i in FAR_FIRST:
            remote(
                own_leg.at[pl.ds(2 * h, 2)], leg.at[pl.ds(2 * h, 2), lev],
                leg_ss.at[h], leg_rs.at[h], (wave, lev_peer(i)),
            )

    def send_spec(e, h):
        for i in FAR_FIRST:
            v = lev_peer(i)
            remote(
                send_f.at[v, e, pl.ds(2 * h, 2)], recv_f.at[e, pl.ds(2 * h, 2), lev],
                lev_ss.at[0, e, h], lev_rs.at[0, e, h], (wave, v),
            )

    send_leg(0)
    send_spec(0, 0)
    send_leg(1)
    send_spec(0, 1)
    send_spec(1, 0)
    send_spec(1, 1)
    for s in range(4):
        leg[s, lev] = own_leg[s]
        for e in range(2):
            recv_f[e, s, lev] = send_f[lev, e, s]

    sub = lax.broadcasted_iota(jnp.int32, (32, 8, 128), 1)

    def interleave(p, q):
        return (
            jnp.where(sub < 4, p, pltpu.roll(q, 4, 1)),
            jnp.where(sub < 4, pltpu.roll(p, 4, 1), q),
        )

    def first_hop(d, e, h, src, by, bz):
        for i in FAR_FIRST:
            if h == 0:
                k = lax.rem(y + i, 8)
                remote(
                    src.at[e, 0, :, k], by.at[e, y],
                    wave_ss.at[d, 0, e, h], wave_rs.at[d, 0, e, h], (z * 8 + k, lev),
                )
            else:
                k = lax.rem(z + i, 8)
                remote(
                    src.at[e, 1, k], bz.at[e, z],
                    wave_ss.at[d, 0, e, h], wave_rs.at[d, 0, e, h], (k * 8 + y, lev),
                )
        if h == 0:
            by[e, y] = src[e, 0, :, y]
        else:
            bz[e, z] = src[e, 1, z]

    def second_hop(d, e, h, by, bz, dst):
        if h == 0:
            arrived(by.at[e, pl.ds(0, 7)], wave_rs.at[d, 0, e, h])
        else:
            arrived(bz.at[e, pl.ds(0, 7)], wave_rs.at[d, 0, e, h])
        for i in FAR_FIRST:
            if h == 0:
                k = lax.rem(z + i, 8)
                remote(
                    by.at[e, :, k], dst.at[e, 0, z],
                    wave_ss.at[d, 1, e, h], wave_rs.at[d, 1, e, h], (k * 8 + y, lev),
                )
            else:
                k = lax.rem(y + i, 8)
                remote(
                    bz.at[e, :, k], dst.at[e, 1, :, y],
                    wave_ss.at[d, 1, e, h], wave_rs.at[d, 1, e, h], (z * 8 + k, lev),
                )
        if h == 0:
            dst[e, 0, z] = by[e, :, z]
        else:
            dst[e, 1, :, y] = bz[e, :, y]

    def legendre(e, h):
        arrived(recv_f.at[e, pl.ds(2 * h, 2), pl.ds(0, 7)], lev_rs.at[0, e, h])
        parts = []
        for s in (2 * h, 2 * h + 1):
            out = dot(leg_t[s], recv_f[e, s].reshape(256, 128))
            parts.append(out.reshape(32, 8, 128))
        low, high = interleave(*parts)
        pairs = jnp.stack([low, high], axis=1).reshape(8, 8, 8, 128)
        a1[e, h] = pairs.astype(BF16)
        first_hop(0, e, h, a1, b1y, b1z)

    def gather_leg(h):
        arrived(leg.at[pl.ds(2 * h, 2), pl.ds(0, 7)], leg_rs.at[h])
        for s in (2 * h, 2 * h + 1):
            leg_t[s] = leg[s].reshape(256, 256).T

    gather_leg(0)
    legendre(0, 0)
    gather_leg(1)
    legendre(0, 1)
    second_hop(0, 0, 0, b1y, b1z, c1)
    legendre(1, 0)
    second_hop(0, 0, 1, b1y, b1z, c1)
    legendre(1, 1)
    second_hop(0, 1, 0, b1y, b1z, c1)
    second_hop(0, 1, 1, b1y, b1z, c1)

    ins[3].wait()
    ins[4].wait()
    diagonal = lax.broadcasted_iota(jnp.int32, (64, 64), 0) == lax.broadcasted_iota(
        jnp.int32, (64, 64), 1
    )
    bands = lax.broadcasted_iota(jnp.int32, (8, 64), 0)
    scales = []
    for t in range(4):
        line = jnp.sum(jnp.where(bands == band_s[t], scale[...], 0.0), axis=0, keepdims=True)
        square = jnp.where(diagonal, jnp.broadcast_to(line, (64, 64)), 0.0)
        scales.append(jnp.sum(square, axis=1, keepdims=True))
    first_half = lax.broadcasted_iota(jnp.int32, (256, 128), 1) < 64

    def grid_point(e):
        arrived(c1.at[e, 0, pl.ds(0, 7)], wave_rs.at[0, 1, e, 0])
        arrived(c1.at[e, 1, pl.ds(0, 7)], wave_rs.at[0, 1, e, 1])
        for h in range(2):
            xf[h] = c1[e, h].astype(F32).reshape(512, 128)
        backs = []
        for t in range(4):
            x = jnp.concatenate([xf[h, pl.ds(t, 128, stride=4), :] for h in range(2)], axis=0)
            xt = x.T.astype(BF16)
            got = dot(xt[0:64], table[t, 0]) + dot(xt[64:128], table[t, 1])
            made = (got * scales[t]).astype(BF16)
            inc[e, t] = made
            heavy = (made.astype(F32) * obs[t].astype(F32) * scales[t]).astype(BF16)
            twice = jnp.concatenate([heavy, heavy], axis=0)
            real = dot(table[t, 0], twice, ((1,), (1,)))
            imag = dot(table[t, 1], twice, ((1,), (1,)))
            backs.append(jnp.where(first_half, real, imag))
        for t in range(4):
            for h in range(2):
                xf[h, pl.ds(t, 128, stride=4), :] = backs[t][h * 128 : h * 128 + 128]
        for h in range(2):
            a2[e, h] = xf[h].reshape(8, 8, 8, 128).astype(BF16)
            first_hop(1, e, h, a2, b2y, b2z)
        pltpu.make_async_copy(inc.at[e], inc_h.at[e], out_sem.at[0, e]).start()

    grid_point(0)
    grid_point(1)
    for e in range(2):
        for h in range(2):
            second_hop(1, e, h, b2y, b2z, c2)

    def legendre_back(e, h):
        if h == 0:
            arrived(c2.at[e, 0, pl.ds(0, 7)], wave_rs.at[1, 1, e, h])
        else:
            arrived(c2.at[e, 1, pl.ds(0, 7)], wave_rs.at[1, 1, e, h])
        rows = c2[e, h].astype(F32).reshape(32, 2, 8, 128)
        for i, piece in enumerate(interleave(rows[:, 0], rows[:, 1])):
            s = 2 * h + i
            out = dot(leg[s].reshape(256, 256), piece.reshape(256, 128).astype(BF16))
            out = out.astype(BF16).reshape(8, 32, 128)
            for v in range(8):
                send_b[v, e, s] = out[v]
        for i in FAR_FIRST:
            v = lev_peer(i)
            remote(
                send_b.at[v, e, pl.ds(2 * h, 2)], recv_b.at[lev, e, pl.ds(2 * h, 2)],
                lev_ss.at[1, e, h], lev_rs.at[1, e, h], (wave, v),
            )
        for s in (2 * h, 2 * h + 1):
            recv_b[lev, e, s] = send_b[lev, e, s]

    def vertical_back(e):
        for h in range(2):
            arrived(recv_b.at[pl.ds(0, 7), e, pl.ds(2 * h, 2)], lev_rs.at[1, e, h])
        for a in range(VARIABLES):
            both = [recv_b[2 * a + half, e].reshape(128, 128) for half in range(2)]
            out = jnp.zeros((128, 256), F32)
            for b in range(COV_BANDS):
                x = jnp.concatenate([part * mask[b] for part in both], axis=1)
                out = out + dot(x, mix[b * VARIABLES + a])
            out = out.astype(BF16)
            grad[e, :, a * 128 : a * 128 + 128] = out[:, 0:128]
            grad[e, :, 512 + a * 128 : 640 + a * 128] = out[:, 128:256]
        pltpu.make_async_copy(grad.at[e], grad_h.at[e], out_sem.at[1, e]).start()

    for h in range(2):
        legendre_back(0, h)
    for h in range(2):
        legendre_back(1, h)
    vertical_back(0)
    vertical_back(1)

    for h in range(2):
        arrived(leg.at[pl.ds(2 * h, 2), pl.ds(0, 7)], leg_ss.at[h])
        for e in range(2):
            for d in range(2):
                arrived(recv_f.at[e, pl.ds(2 * h, 2), pl.ds(0, 7)], lev_ss.at[d, e, h])
                for hop in range(2):
                    arrived(b1y.at[e, pl.ds(0, 7)], wave_ss.at[d, hop, e, h])
    for e in range(2):
        pltpu.make_async_copy(inc.at[e], inc_h.at[e], out_sem.at[0, e]).wait()
        pltpu.make_async_copy(grad.at[e], grad_h.at[e], out_sem.at[1, e]).wait()


def shards(control, wave_of_slot, legendre, vertical, points, lat_band, grid_scale, obs_weight):
    members, slots, rows_dev = control.shape[0], control.shape[1], control.shape[2]
    flat = control.reshape(members * slots * rows_dev, 1024)
    smem = pl.BlockSpec(memory_space=pltpu.SMEM)
    vmem = pl.BlockSpec(memory_space=pltpu.VMEM)
    anywhere = pl.BlockSpec(memory_space=pl.ANY)
    wide = (2, 2, 8, 8, 8, 128)
    hop = (2, 8, 8, 8, 128)
    increment, gradient = pl.pallas_call(
        kernel,
        out_shape=(
            jax.ShapeDtypeStruct((2, 4, 64, 512), BF16),
            jax.ShapeDtypeStruct((2, 128, 1024), BF16),
        ),
        in_specs=[smem, smem, smem, vmem] + [anywhere] * 5,
        out_specs=(anywhere, anywhere),
        scratch_shapes=[
            pltpu.VMEM((256, 1024), BF16),
            pltpu.VMEM((16, 128, 128), BF16),
            pltpu.VMEM((4, 32, 256), BF16),
            pltpu.VMEM((8, 64), F32),
            pltpu.VMEM((4, 64, 512), BF16),
            pltpu.VMEM((2, 4, 64, 512), BF16),
            pltpu.VMEM((2, 128, 1024), BF16),
            pltpu.VMEM((4, 128, 128), BF16),
            pltpu.VMEM((16, 256, 256), BF16),
            pltpu.VMEM((8, 2, 4, 32, 128), BF16),
            pltpu.VMEM((2, 4, 8, 32, 128), BF16),
            pltpu.VMEM((4, 8, 32, 256), BF16),
            pltpu.VMEM((4, 256, 256), BF16),
            pltpu.VMEM((256, 128), F32),
            pltpu.VMEM((4, 2, 256, 512), BF16),
            pltpu.VMEM(wide, BF16),
            pltpu.VMEM(hop, BF16),
            pltpu.VMEM(hop, BF16),
            pltpu.VMEM(wide, BF16),
            pltpu.VMEM((2, 512, 128), F32),
            pltpu.VMEM(wide, BF16),
            pltpu.VMEM(hop, BF16),
            pltpu.VMEM(hop, BF16),
            pltpu.VMEM(wide, BF16),
            pltpu.VMEM((8, 2, 4, 32, 128), BF16),
            pltpu.VMEM((8, 2, 4, 32, 128), BF16),
            pltpu.SemaphoreType.DMA((5,)),
            pltpu.SemaphoreType.DMA((2, 2)),
            pltpu.SemaphoreType.DMA((2,)),
            pltpu.SemaphoreType.DMA((2,)),
            pltpu.SemaphoreType.DMA((2, 2, 2)),
            pltpu.SemaphoreType.DMA((2, 2, 2)),
            pltpu.SemaphoreType.DMA((2, 2, 2, 2)),
            pltpu.SemaphoreType.DMA((2, 2, 2, 2)),
        ],
        compiler_params=pltpu.CompilerParams(
            collective_id=0, has_side_effects=True, vmem_limit_bytes=60_000_000
        ),
    )(
        wave_of_slot, points, lat_band, wave_of_slot.reshape(2, 128),
        flat, legendre, vertical.reshape(16, 128, 128), grid_scale, obs_weight,
    )
    return increment, gradient.reshape(control.shape)


def solution(mesh):
    in_specs = (
        P(None, "wave", "lev", None, None),
        P(),
        P("wave", "lev", None),
        P(),
        P("wave"),
        P("wave"),
        P(None, "lev"),
        P("wave", "lev", None),
    )
    out_specs = (P(None, "wave", "lev", None), P(None, "wave", "lev", None, None))
    return jax.shard_map(shards, mesh=mesh, in_specs=in_specs, out_specs=out_specs, check_vma=False)
```

time: 146 us -> 72.3 us (0.50)
  Pallas kernels: 0 us -> 66.4 us
  blocking collectives: 46.3 us -> 0 us
  other arithmetic: 30.1 us -> 0 us
  starting transfers between devices: 25.8 us -> 0 us
  local copies, waits for them, and re-layouts: 23 us -> 4.99 us
  waiting for transfers between devices: 12.3 us -> 0 us
  matrix products: 7.04 us -> 0 us
    pallas_call x0 -> x1, Pallas kernels: none -> 66.4 us  [shards(): pl.pallas_call(kernel, out_shape=(jax.ShapeDtypeStruct((2, 4, 64, 512), B...]
    all_to_all x2 -> x0, blocking collectives: 46.3 us -> none  [the longest x1 27.8 us: to_bands(): lax.all_to_all(values, 'wave', split_axis=2, concat_axis=1, tiled=True)]
    another operation x1 -> x0, other arithmetic: 28.9 us -> none
    all_to_all x3 -> x0, starting transfers between devices: 25.8 us -> none  [the longest x1 12.8 us: to_bands(): lax.all_to_all(values, 'wave', split_axis=2, concat_axis=1, tiled=True)]
    all_to_all x3 -> x0, waiting for transfers between devices: 12.3 us -> none  [the longest x1 8.55 us: shards(): lax.all_to_all(adjoint_coeffs, 'lev', split_axis=2, concat_axis=4, tiled=...]
    dot_general x13 -> x0, matrix products: 7.04 us -> none  [the longest x8 3.35 us: vertical_apply(): jnp.einsum(form, shaped, vertical[index_band], preferred_element_type=jnp...]
    unnamed x31 -> x4, local copies, waits for them, and re-layouts: 7.72 us -> 2.71 us
    all_to_all x7 -> x0, local copies, waits for them, and re-layouts: 4.39 us -> none  [the longest x1 2.97 us: shards(): lax.all_to_all(spectral, 'lev', split_axis=4, concat_axis=2, tiled=True)]
  transfers between devices with their start and end apart: 3 -> 0, of which waited for: 2 -> 0; matrix products, arithmetic and copies ran while one was open for 25% -> 0% of each run, Pallas kernels for 0% -> 0%
where the time goes in v1:
time: 72.3 us; the launch traced here: 72.1 us
  Pallas kernels  66.4 us (92%)
  local copies, waits for them, and re-layouts  4.99 us (7%)
    pallas_call x1, Pallas kernels, shards(): pl.pallas_call(kernel, out_shape=(jax.ShapeDtypeStruct((2, 4, 64, 512), B...  66.4 us
    unnamed x4, local copies, waits for them, and re-layouts  2.71 us
    reshape x1, local copies, waits for them, and re-layouts, shards(): return (increment, gradient.reshape(control.shape))  2.28 us

profile of v1, /device:TPU:1, one launch (start us, length us, event | category | flops | bytes accessed | tf_op | source)
XLA Modules:
  0.0 72.1 jit_solution(8188878316495243330)
XLA Ops:
  0.6 1.9 %copy.10 = bf16[32,8,2,512]{3,1,2,0:T(8,128)(2,1)} copy(bf16[32,8,2,512]{3,2,1,0:T(2,128)(2,1)} %bitcast.7) | data formatting | bytes 1048576
  2.5 66.4 %shard_map.95 = (bf16[2,4,64,512]{3,2,1,0:T(8,128)(2,1)}, bf16[2,128,1024]{2,1,0:T(8,128)(2,1)}) custom-call(s32[256]{0:T(256)} %waves_s.1, s32[4]{0:T(128)} %points_s.1, s32[4]{0:T(128)} %band_s.1, s32[2,128]{1,0:T(2,128)} %bitcast.8, bf16[256,1024]{1,0:T(8,128)(2,1)} %bitcast.5, bf16[4,32,256]{2,1,0:T(8,128)(2,1)} %leg_h.1, bf16[16,128,128]{2,1,0:T(8,128)(2,1)} %bitcast.6, ...), custom_call_target="tpu_custom_call" | custom-call | tf_op jit(solution)/shard_map/pallas_call | solution.py:360
  69.0 0.0 copy-start
  69.0 2.3 %reshape.19 = bf16[2,4,32,2,512]{4,3,2,1,0:T(2,128)(2,1)} reshape(bf16[2,128,1024]{2,1,0:T(8,128)(2,1)} %get-tuple-element.5) | data formatting | bytes 1048576 | tf_op jit(solution)/shard_map/reshape | solution.py:411
  71.3 0.0 copy-done
  71.3 0.8 %copy.12 = bf16[2,4,64,512]{3,2,1,0:T(8,128)(2,1)} copy(bf16[2,4,64,512]{3,2,1,0:T(8,128)(2,1)S(1)} %copy-done) | data formatting | bytes 1048576
Async XLA Ops:
  69.0 2.3 %copy-start = (bf16[2,4,64,512]{3,2,1,0:T(8,128)(2,1)S(1)}, bf16[2,4,64,512]{3,2,1,0:T(8,128)(2,1)}, u32[]{:S(2)}) copy-start(bf16[2,4,64,512]{3,2,1,0:T(8,128)(2,1)} %get-tuple-element.8) | copy-start | bytes 1572868

commit v2 on v1

--- a/solution.py
+++ b/solution.py
@@ -33,26 +33,16 @@
 
 
 def kernel(
-    waves_s, points_s, band_s, waves_v, ctl_h, leg_h, ver_h, scale_h, obs_h,
-    inc_h, grad_h,
-    ctl, ver, own_leg, scale, obs, inc, grad,
+    waves_s, points_s, band_s, waves_v, ctl, own_leg, ver, scale, obs,
+    inc, grad,
     mask, mix, send_f, recv_f, leg, leg_t, wcol, table,
-    a1, b1y, b1z, c1, xf, a2, b2y, b2z, c2, send_b, recv_b,
-    in_sem, out_sem, leg_ss, leg_rs, lev_ss, lev_rs, wave_ss, wave_rs,
+    a1, c1, xf, a2, c2, send_b, recv_b,
+    ready, leg_ss, leg_rs, lev_ss, lev_rs, wave_ss, wave_rs,
 ):
     wave = lax.axis_index("wave")
     lev = lax.axis_index("lev")
     z = wave // 8
     y = lax.rem(wave, 8)
-
-    ins = [
-        pltpu.make_async_copy(src, dst, in_sem.at[i])
-        for i, (src, dst) in enumerate(
-            ((ctl_h, ctl), (ver_h, ver), (leg_h, own_leg), (scale_h, scale), (obs_h, obs))
-        )
-    ]
-    for copy in ins:
-        copy.start()
 
     barrier = pltpu.get_barrier_semaphore()
 
@@ -76,8 +66,6 @@
     for b in range(COV_BANDS):
         chosen = (total <= WAVES - 1) & (band == b)
         mask[b] = jnp.where(chosen, 1.0, 0.0).astype(BF16)
-
-    ins[1].wait()
 
     def lay(i, carry):
         zero = jnp.zeros((64, 128), BF16)
@@ -92,7 +80,6 @@
 
     lax.fori_loop(0, COV_BANDS * VARIABLES, lay, 0)
 
-    ins[0].wait()
     for a in range(VARIABLES):
         both = [ctl[:, a * 128 : a * 128 + 128], ctl[:, 512 + a * 128 : 640 + a * 128]]
         out = jnp.zeros((256, 256), F32)
@@ -103,6 +90,49 @@
         out = out.astype(BF16)
         for half in range(2):
             send_f[2 * a + half] = out[:, half * 128 : half * 128 + 128].reshape(2, 4, 32, 128)
+
+    pl.semaphore_wait(barrier, 21)
+    for i in FAR_FIRST:
+        pl.semaphore_signal(
+            ready, inc=1, device_id=(lax.rem(z + i, 8) * 8 + y, lev), device_id_type=MESH
+        )
+
+    def lev_peer(i):
+        return lax.rem(lev + i, 8)
+
+    def remote(src, dst, ss, rs, who):
+        pltpu.make_async_remote_copy(
+            src, dst, ss, rs, device_id=who, device_id_type=MESH
+        ).start()
+
+    def arrived(buffer, sem):
+        pltpu.make_async_copy(buffer, buffer, sem).wait()
+
+    def send_leg(h):
+        for i in FAR_FIRST:
+            remote(
+                own_leg.at[pl.ds(2 * h, 2)], leg.at[pl.ds(2 * h, 2), lev],
+                leg_ss.at[h], leg_rs.at[h], (wave, lev_peer(i)),
+            )
+
+    def send_spec(e, h):
+        for i in FAR_FIRST:
+            v = lev_peer(i)
+            remote(
+                send_f.at[v, e, pl.ds(2 * h, 2)], recv_f.at[e, pl.ds(2 * h, 2), lev],
+                lev_ss.at[0, e, h], lev_rs.at[0, e, h], (wave, v),
+            )
+
+    send_leg(0)
+    send_spec(0, 0)
+    send_leg(1)
+    send_spec(0, 1)
+    send_spec(1, 0)
+    send_spec(1, 1)
+    for s in range(4):
+        leg[s, lev] = own_leg[s]
+        for e in range(2):
+            recv_f[e, s, lev] = send_f[lev, e, s]
 
     place = lax.broadcasted_iota(jnp.int32, (256, 128), 0)
     wanted = lax.rem(place, 128) // 2 * 4 + place // 128 * 2 + lax.rem(place, 2)
@@ -134,46 +164,6 @@
 
         lax.fori_loop(0, 16, rows_of_table, 0)
 
-    ins[2].wait()
-    pl.semaphore_wait(barrier, 21)
-
-    def lev_peer(i):
-        return lax.rem(lev + i, 8)
-
-    def remote(src, dst, ss, rs, who):
-        pltpu.make_async_remote_copy(
-            src, dst, ss, rs, device_id=who, device_id_type=MESH
-        ).start()
-
-    def arrived(buffer, sem):
-        pltpu.make_async_copy(buffer, buffer, sem).wait()
-
-    def send_leg(h):
-        for i in FAR_FIRST:
-            remote(
-                own_leg.at[pl.ds(2 * h, 2)], leg.at[pl.ds(2 * h, 2), lev],
-                leg_ss.at[h], leg_rs.at[h], (wave, lev_peer(i)),
-            )
-
-    def send_spec(e, h):
-        for i in FAR_FIRST:
-            v = lev_peer(i)
-            remote(
-                send_f.at[v, e, pl.ds(2 * h, 2)], recv_f.at[e, pl.ds(2 * h, 2), lev],
-                lev_ss.at[0, e, h], lev_rs.at[0, e, h], (wave, v),
-            )
-
-    send_leg(0)
-    send_spec(0, 0)
-    send_leg(1)
-    send_spec(0, 1)
-    send_spec(1, 0)
-    send_spec(1, 1)
-    for s in range(4):
-        leg[s, lev] = own_leg[s]
-        for e in range(2):
-            recv_f[e, s, lev] = send_f[lev, e, s]
-
     sub = lax.broadcasted_iota(jnp.int32, (32, 8, 128), 1)
 
     def interleave(p, q):
@@ -182,47 +172,20 @@
             jnp.where(sub < 4, pltpu.roll(p, 4, 1), q),
         )
 
-    def first_hop(d, e, h, src, by, bz):
-        for i in FAR_FIRST:
-            if h == 0:
-                k = lax.rem(y + i, 8)
-                remote(
-                    src.at[e, 0, :, k], by.at[e, y],
-                    wave_ss.at[d, 0, e, h], wave_rs.at[d, 0, e, h], (z * 8 + k, lev),
-                )
-            else:
-                k = lax.rem(z + i, 8)
-                remote(
-                    src.at[e, 1, k], bz.at[e, z],
-                    wave_ss.at[d, 0, e, h], wave_rs.at[d, 0, e, h], (k * 8 + y, lev),
-                )
-        if h == 0:
-            by[e, y] = src[e, 0, :, y]
-        else:
-            bz[e, z] = src[e, 1, z]
-
-    def second_hop(d, e, h, by, bz, dst):
-        if h == 0:
-            arrived(by.at[e, pl.ds(0, 7)], wave_rs.at[d, 0, e, h])
-        else:
-            arrived(bz.at[e, pl.ds(0, 7)], wave_rs.at[d, 0, e, h])
-        for i in FAR_FIRST:
-            if h == 0:
-                k = lax.rem(z + i, 8)
-                remote(
-                    by.at[e, :, k], dst.at[e, 0, z],
-                    wave_ss.at[d, 1, e, h], wave_rs.at[d, 1, e, h], (k * 8 + y, lev),
-                )
-            else:
-                k = lax.rem(y + i, 8)
-                remote(
-                    bz.at[e, :, k], dst.at[e, 1, :, y],
-                    wave_ss.at[d, 1, e, h], wave_rs.at[d, 1, e, h], (z * 8 + k, lev),
-                )
-        if h == 0:
-            dst[e, 0, z] = by[e, :, z]
-        else:
-            dst[e, 1, :, y] = bz[e, :, y]
+    def exchange(d, e, h, src, dst):
+        def one(i, carry):
+            k = lax.rem(wave + i, 64)
+            remote(
+                src.at[e, h, k], dst.at[e, h, wave],
+                wave_ss.at[d, e, h], wave_rs.at[d, e, h], (k, lev),
+            )
+            return carry
+
+        lax.fori_loop(1, 64, one, 0, unroll=7)
+        dst[e, h, wave] = src[e, h, wave]
+
+    def exchanged(d, e, h, dst):
+        arrived(dst.at[e, h, pl.ds(0, 63)], wave_rs.at[d, e, h])
 
     def legendre(e, h):
         arrived(recv_f.at[e, pl.ds(2 * h, 2), pl.ds(0, 7)], lev_rs.at[0, e, h])
@@ -231,9 +194,9 @@
             out = dot(leg_t[s], recv_f[e, s].reshape(256, 128))
             parts.append(out.reshape(32, 8, 128))
         low, high = interleave(*parts)
-        pairs = jnp.stack([low, high], axis=1).reshape(8, 8, 8, 128)
+        pairs = jnp.stack([low, high], axis=1).reshape(64, 8, 128)
         a1[e, h] = pairs.astype(BF16)
-        first_hop(0, e, h, a1, b1y, b1z)
+        exchange(0, e, h, a1, c1)
 
     def gather_leg(h):
         arrived(leg.at[pl.ds(2 * h, 2), pl.ds(0, 7)], leg_rs.at[h])
@@ -241,18 +204,13 @@
             leg_t[s] = leg[s].reshape(256, 256).T
 
     gather_leg(0)
+    pl.semaphore_wait(ready, 7)
     legendre(0, 0)
     gather_leg(1)
     legendre(0, 1)
-    second_hop(0, 0, 0, b1y, b1z, c1)
     legendre(1, 0)
-    second_hop(0, 0, 1, b1y, b1z, c1)
     legendre(1, 1)
-    second_hop(0, 1, 0, b1y, b1z, c1)
-    second_hop(0, 1, 1, b1y, b1z, c1)
-
-    ins[3].wait()
-    ins[4].wait()
+
     diagonal = lax.broadcasted_iota(jnp.int32, (64, 64), 0) == lax.broadcasted_iota(
         jnp.int32, (64, 64), 1
     )
@@ -265,9 +223,8 @@
     first_half = lax.broadcasted_iota(jnp.int32, (256, 128), 1) < 64
 
     def grid_point(e):
-        arrived(c1.at[e, 0, pl.ds(0, 7)], wave_rs.at[0, 1, e, 0])
-        arrived(c1.at[e, 1, pl.ds(0, 7)], wave_rs.at[0, 1, e, 1])
         for h in range(2):
+            exchanged(0, e, h, c1)
             xf[h] = c1[e, h].astype(F32).reshape(512, 128)
         backs = []
         for t in range(4):
@@ -285,21 +242,13 @@
             for h in range(2):
                 xf[h, pl.ds(t, 128, stride=4), :] = backs[t][h * 128 : h * 128 + 128]
         for h in range(2):
-            a2[e, h] = xf[h].reshape(8, 8, 8, 128).astype(BF16)
-            first_hop(1, e, h, a2, b2y, b2z)
-        pltpu.make_async_copy(inc.at[e], inc_h.at[e], out_sem.at[0, e]).start()
+            a2[e, h] = xf[h].reshape(64, 8, 128).astype(BF16)
+            exchange(1, e, h, a2, c2)
 
     grid_point(0)
     grid_point(1)
-    for e in range(2):
-        for h in range(2):
-            second_hop(1, e, h, b2y, b2z, c2)
-
     def legendre_back(e, h):
-        if h == 0:
-            arrived(c2.at[e, 0, pl.ds(0, 7)], wave_rs.at[1, 1, e, h])
-        else:
-            arrived(c2.at[e, 1, pl.ds(0, 7)], wave_rs.at[1, 1, e, h])
+        exchanged(1, e, h, c2)
         rows = c2[e, h].astype(F32).reshape(32, 2, 8, 128)
         for i, piece in enumerate(interleave(rows[:, 0], rows[:, 1])):
             s = 2 * h + i
@@ -328,7 +277,6 @@
             out = out.astype(BF16)
             grad[e, :, a * 128 : a * 128 + 128] = out[:, 0:128]
             grad[e, :, 512 + a * 128 : 640 + a * 128] = out[:, 128:256]
-        pltpu.make_async_copy(grad.at[e], grad_h.at[e], out_sem.at[1, e]).start()
 
     for h in range(2):
         legendre_back(0, h)
@@ -342,11 +290,7 @@
         for e in range(2):
             for d in range(2):
                 arrived(recv_f.at[e, pl.ds(2 * h, 2), pl.ds(0, 7)], lev_ss.at[d, e, h])
-                for hop in range(2):
-                    arrived(b1y.at[e, pl.ds(0, 7)], wave_ss.at[d, hop, e, h])
-    for e in range(2):
-        pltpu.make_async_copy(inc.at[e], inc_h.at[e], out_sem.at[0, e]).wait()
-        pltpu.make_async_copy(grad.at[e], grad_h.at[e], out_sem.at[1, e]).wait()
+                arrived(c1.at[e, h, pl.ds(0, 63)], wave_ss.at[d, e, h])
 
 
 def shards(control, wave_of_slot, legendre, vertical, points, lat_band, grid_scale, obs_weight):
@@ -354,25 +298,16 @@
     flat = control.reshape(members * slots * rows_dev, 1024)
     smem = pl.BlockSpec(memory_space=pltpu.SMEM)
     vmem = pl.BlockSpec(memory_space=pltpu.VMEM)
-    anywhere = pl.BlockSpec(memory_space=pl.ANY)
-    wide = (2, 2, 8, 8, 8, 128)
-    hop = (2, 8, 8, 8, 128)
+    wide = (2, 2, 64, 8, 128)
     increment, gradient = pl.pallas_call(
         kernel,
         out_shape=(
             jax.ShapeDtypeStruct((2, 4, 64, 512), BF16),
             jax.ShapeDtypeStruct((2, 128, 1024), BF16),
         ),
-        in_specs=[smem, smem, smem, vmem] + [anywhere] * 5,
-        out_specs=(anywhere, anywhere),
+        in_specs=[smem] * 3 + [vmem] * 6,
+        out_specs=(vmem, vmem),
         scratch_shapes=[
-            pltpu.VMEM((256, 1024), BF16),
-            pltpu.VMEM((16, 128, 128), BF16),
-            pltpu.VMEM((4, 32, 256), BF16),
-            pltpu.VMEM((8, 64), F32),
-            pltpu.VMEM((4, 64, 512), BF16),
-            pltpu.VMEM((2, 4, 64, 512), BF16),
-            pltpu.VMEM((2, 128, 1024), BF16),
             pltpu.VMEM((4, 128, 128), BF16),
             pltpu.VMEM((16, 256, 256), BF16),
             pltpu.VMEM((8, 2, 4, 32, 128), BF16),
@@ -382,27 +317,22 @@
             pltpu.VMEM((256, 128), F32),
             pltpu.VMEM((4, 2, 256, 512), BF16),
             pltpu.VMEM(wide, BF16),
-            pltpu.VMEM(hop, BF16),
-            pltpu.VMEM(hop, BF16),
             pltpu.VMEM(wide, BF16),
             pltpu.VMEM((2, 512, 128), F32),
             pltpu.VMEM(wide, BF16),
-            pltpu.VMEM(hop, BF16),
-            pltpu.VMEM(hop, BF16),
             pltpu.VMEM(wide, BF16),
             pltpu.VMEM((8, 2, 4, 32, 128), BF16),
             pltpu.VMEM((8, 2, 4, 32, 128), BF16),
-            pltpu.SemaphoreType.DMA((5,)),
-            pltpu.SemaphoreType.DMA((2, 2)),
+            pltpu.SemaphoreType.REGULAR,
             pltpu.SemaphoreType.DMA((2,)),
             pltpu.SemaphoreType.DMA((2,)),
             pltpu.SemaphoreType.DMA((2, 2, 2)),
             pltpu.SemaphoreType.DMA((2, 2, 2)),
-            pltpu.SemaphoreType.DMA((2, 2, 2, 2)),
-            pltpu.SemaphoreType.DMA((2, 2, 2, 2)),
+            pltpu.SemaphoreType.DMA((2, 2, 2)),
+            pltpu.SemaphoreType.DMA((2, 2, 2)),
         ],
         compiler_params=pltpu.CompilerParams(
-            collective_id=0, has_side_effects=True, vmem_limit_bytes=60_000_000
+            collective_id=0, has_side_effects=True, vmem_limit_bytes=24_000_000
         ),
     )(
         wave_of_slot, points, lat_band, wave_of_slot.reshape(2, 128),

time: 72.3 us -> 64 us (0.89)
  Pallas kernels: 66.4 us -> 59.3 us
  local copies, waits for them, and re-layouts: 4.99 us -> 3.78 us
    pallas_call x1, Pallas kernels: 66.4 us -> 59.3 us  [shards(): pl.pallas_call(kernel, out_shape=(jax.ShapeDtypeStruct((2, 4, 64, 512), B...]
    reshape x1, local copies, waits for them, and re-layouts: 2.28 us -> 1.17 us  [shards(): return (increment, gradient.reshape(control.shape))]
    unnamed x4 -> x16, local copies, waits for them, and re-layouts: 2.71 us -> 2.61 us
where the time goes in v2:
time: 64 us; the launch traced here: 63.8 us
  Pallas kernels  59.3 us (93%)
  local copies, waits for them, and re-layouts  3.78 us (6%)
  between operations  0.74 us (1%)
    pallas_call x1, Pallas kernels, shards(): pl.pallas_call(kernel, out_shape=(jax.ShapeDtypeStruct((2, 4, 64, 512), B...  59.3 us
    unnamed x16, local copies, waits for them, and re-layouts  2.61 us

profile of v2, /device:TPU:1, one launch (start us, length us, event | category | flops | bytes accessed | tf_op | source)
XLA Modules:
  0.0 63.8 jit_solution(11893287464294787084)
XLA Ops:
  0.6 0.0 copy-start
  0.6 0.0 copy-start.1
  0.7 0.0 copy-start.2
  0.7 0.0 copy-start.3
  0.7 0.0 copy-start.6
  0.7 1.2 %copy.10 = bf16[32,8,2,512]{3,1,2,0:T(8,128)(2,1)S(1)} copy(bf16[32,8,2,512]{3,2,1,0:T(2,128)(2,1)} %bitcast.8) | data formatting | bytes 1048576
  1.9 0.0 copy-start.4
  1.9 0.0 copy-start.5
  1.9 0.0 copy-done
  1.9 0.0 copy-done.1
  1.9 0.0 copy-done.2
  1.9 0.0 copy-done.3
  1.9 0.0 copy-done.6
  1.9 0.6 copy-done.4
  2.6 0.0 copy-done.5
  2.6 59.3 %shard_map.95 = (bf16[2,4,64,512]{3,2,1,0:T(8,128)(2,1)S(1)}, bf16[2,128,1024]{2,1,0:T(8,128)(2,1)S(1)}) custom-call(s32[256]{0:T(256)S(1)} %copy-done.4, s32[4]{0:T(128)S(1)} %copy-done.5, s32[4]{0:T(128)S(1)} %copy-done.6, s32[2,128]{1,0:T(2,128)S(1)} %bitcast.7, bf16[256,1024]{1,0:T(8,128)(2,1)S(1)} %bitcast.5, bf16[4,32,256]{2,1,0:T(8,128)(2,1)S(1)} %copy-done.2, ...), custom_call_target="tpu_custom_call" | custom-call | tf_op jit(solution)/shard_map/pallas_call | solution.py:302
  61.9 1.2 %reshape.19 = bf16[2,4,32,2,512]{4,3,2,1,0:T(2,128)(2,1)} reshape(bf16[2,128,1024]{2,1,0:T(8,128)(2,1)S(1)} %get-tuple-element.5) | data formatting | bytes 1048576 | tf_op jit(solution)/shard_map/reshape | solution.py:341
  63.0 0.8 %copy.12 = bf16[2,4,64,512]{3,2,1,0:T(8,128)(2,1)} copy(bf16[2,4,64,512]{3,2,1,0:T(8,128)(2,1)S(1)} %get-tuple-element.8) | data formatting | bytes 1048576
Async XLA Ops:
  0.6 1.3 %copy-start = (bf16[4,4,128,128]{3,2,1,0:T(8,128)(2,1)S(1)}, bf16[4,4,128,128]{3,2,1,0:T(8,128)(2,1)}, u32[]{:S(2)}) copy-start(bf16[4,4,128,128]{3,2,1,0:T(8,128)(2,1)} %param.11) | copy-start | bytes 1572868
  0.6 1.3 %copy-start.1 = (bf16[4,64,512]{2,1,0:T(8,128)(2,1)S(1)}, bf16[4,64,512]{2,1,0:T(8,128)(2,1)}, u32[]{:S(2)}) copy-start(bf16[4,64,512]{2,1,0:T(8,128)(2,1)} %obs.1) | copy-start | bytes 786436
  0.7 1.3 %copy-start.2 = (bf16[4,32,256]{2,1,0:T(8,128)(2,1)S(1)}, bf16[4,32,256]{2,1,0:T(8,128)(2,1)}, u32[]{:S(2)}) copy-start(bf16[4,32,256]{2,1,0:T(8,128)(2,1)} %own_leg.1) | copy-start | bytes 196612
  0.7 1.3 %copy-start.3 = (f32[8,64]{1,0:T(8,128)S(1)}, f32[8,64]{1,0:T(8,128)}, u32[]{:S(2)}) copy-start(f32[8,64]{1,0:T(8,128)} %scale.1) | copy-start | bytes 6148
  0.7 1.3 %copy-start.6 = (s32[4]{0:T(128)S(1)}, s32[4]{0:T(128)}, u32[]{:S(2)}) copy-start(s32[4]{0:T(128)} %band_s.1) | copy-start | bytes 52
  1.9 0.7 %copy-start.4 = (s32[256]{0:T(256)S(1)}, s32[256]{0:T(256)}, u32[]{:S(2)}) copy-start(s32[256]{0:T(256)} %waves_s.1) | copy-start | bytes 3076
  1.9 0.7 %copy-start.5 = (s32[4]{0:T(128)S(1)}, s32[4]{0:T(128)}, u32[]{:S(2)}) copy-start(s32[4]{0:T(128)} %points_s.1) | copy-start | bytes 52

commit v3 on v2

--- a/solution.py
+++ b/solution.py
@@ -33,39 +33,44 @@
 
 
 def kernel(
-    waves_s, points_s, band_s, waves_v, ctl, own_leg, ver, scale, obs,
+    waves_h, points_h, band_h, ctl, own_leg, ver, scale, obs,
     inc, grad,
-    mask, mix, send_f, recv_f, leg, leg_t, wcol, table,
+    waves_v, points_v, band_v, mask, mix, send_f, recv_f, leg, leg_t, wcol, table,
     a1, c1, xf, a2, c2, send_b, recv_b,
-    ready, leg_ss, leg_rs, lev_ss, lev_rs, wave_ss, wave_rs,
+    in_sem, near, row_col, plane, leg_ss, leg_rs, leg_ps, lev_ss, lev_rs, wave_ss, wave_rs,
 ):
     wave = lax.axis_index("wave")
     lev = lax.axis_index("lev")
     z = wave // 8
     y = lax.rem(wave, 8)
 
+    small = [
+        pltpu.make_async_copy(src, dst, in_sem.at[i])
+        for i, (src, dst) in enumerate(
+            ((waves_h, waves_v), (points_h, points_v), (band_h, band_v))
+        )
+    ]
+    for copy in small:
+        copy.start()
     barrier = pltpu.get_barrier_semaphore()
 
-    def along(i):
-        return (
-            (wave, lax.rem(lev + i, 8)),
-            (z * 8 + lax.rem(y + i, 8), lev),
-            (lax.rem(z + i, 8) * 8 + y, lev),
-        )
+    def greet(sem, who):
+        pl.semaphore_signal(sem, inc=1, device_id=who, device_id_type=MESH)
+
+    def on_y(i):
+        return (z * 8 + lax.rem(y + i, 8), lev)
+
+    def on_z(i):
+        return (lax.rem(z + i, 8) * 8 + y, lev)
+
+    def lev_peer(i):
+        return lax.rem(lev + i, 8)
 
     for i in FAR_FIRST:
-        for who in along(i):
-            pl.semaphore_signal(barrier, inc=1, device_id=who, device_id_type=MESH)
-
-    row = lax.broadcasted_iota(jnp.int32, (128, 128), 0)
-    slot = row // 32
-    total = lev * 32 + lax.rem(row, 32)
-    for s in range(4):
-        total = total + jnp.where(slot == s, waves_s[wave * 4 + s], 0)
-    band = jnp.minimum(total * COV_BANDS // WAVES, COV_BANDS - 1)
-    for b in range(COV_BANDS):
-        chosen = (total <= WAVES - 1) & (band == b)
-        mask[b] = jnp.where(chosen, 1.0, 0.0).astype(BF16)
+        greet(barrier, (wave, lev_peer(i)))
+    for i in (1, 7):
+        greet(barrier, on_y(i))
+        greet(barrier, on_z(i))
 
     def lay(i, carry):
         zero = jnp.zeros((64, 128), BF16)
@@ -80,6 +85,22 @@
 
     lax.fori_loop(0, COV_BANDS * VARIABLES, lay, 0)
 
+    for copy in small:
+        copy.wait()
+
+    row = lax.broadcasted_iota(jnp.int32, (128, 128), 0)
+    slot = row // 32
+    total = lev * 32 + lax.rem(row, 32)
+    numbers = jnp.concatenate([waves_v[0:1, :], waves_v[1:2, :]], axis=1)
+    at_slot = lax.broadcasted_iota(jnp.int32, (1, WAVES), 1) - wave * 4
+    for s in range(4):
+        own = jnp.sum(jnp.where(at_slot == s, numbers.astype(F32), 0.0), axis=1, keepdims=True)
+        total = total + jnp.where(slot == s, own.astype(jnp.int32), 0)
+    band = jnp.minimum(total * COV_BANDS // WAVES, COV_BANDS - 1)
+    for b in range(COV_BANDS):
+        chosen = (total <= WAVES - 1) & (band == b)
+        mask[b] = jnp.where(chosen, 1.0, 0.0).astype(BF16)
+
     for a in range(VARIABLES):
         both = [ctl[:, a * 128 : a * 128 + 128], ctl[:, 512 + a * 128 : 640 + a * 128]]
         out = jnp.zeros((256, 256), F32)
@@ -91,14 +112,10 @@
         for half in range(2):
             send_f[2 * a + half] = out[:, half * 128 : half * 128 + 128].reshape(2, 4, 32, 128)
 
-    pl.semaphore_wait(barrier, 21)
-    for i in FAR_FIRST:
-        pl.semaphore_signal(
-            ready, inc=1, device_id=(lax.rem(z + i, 8) * 8 + y, lev), device_id_type=MESH
-        )
-
-    def lev_peer(i):
-        return lax.rem(lev + i, 8)
+    pl.semaphore_wait(barrier, 11)
+    for i in (1, 7):
+        greet(near, on_y(i))
+        greet(near, on_z(i))
 
     def remote(src, dst, ss, rs, who):
         pltpu.make_async_remote_copy(
@@ -108,11 +125,28 @@
     def arrived(buffer, sem):
         pltpu.make_async_copy(buffer, buffer, sem).wait()
 
+    partner = lev + 1 - 2 * lax.rem(lev, 2)
+
     def send_leg(h):
-        for i in FAR_FIRST:
+        two = pl.ds(2 * h, 2)
+        for i in (4, 2, 6):
             remote(
-                own_leg.at[pl.ds(2 * h, 2)], leg.at[pl.ds(2 * h, 2), lev],
+                own_leg.at[two], leg.at[two, lev],
                 leg_ss.at[h], leg_rs.at[h], (wave, lev_peer(i)),
+            )
+        remote(
+            own_leg.at[two], leg.at[two, lev],
+            leg_ss.at[h], leg_ps.at[h], (wave, partner),
+        )
+
+    def relay_leg(h):
+        two = pl.ds(2 * h, 2)
+        arrived(leg.at[two, pl.ds(0, 3)], leg_rs.at[h])
+        for i in (2, 6, 4):
+            v = lev_peer(i)
+            remote(
+                leg.at[two, v], leg.at[two, v],
+                leg_ss.at[h], leg_ps.at[h], (wave, partner),
             )
 
     def send_spec(e, h):
@@ -143,11 +177,11 @@
         found = found + jnp.where(wanted == lane + i * 128, numbers, 0.0)
     wcol[...] = jnp.broadcast_to(jnp.sum(found, axis=1, keepdims=True), (256, 128))
 
-    for t in range(4):
-        count = jnp.full((16, LONGITUDES), points_s[t], jnp.int32).astype(F32)
+    def make_table(t):
+        count = jnp.broadcast_to(points_v[:, t : t + 1].astype(F32), (16, LONGITUDES))
         inverse = 1.0 / count
 
-        def rows_of_table(i, carry, t=t, count=count, inverse=inverse):
+        def rows_of_table(i, carry):
             at = pl.multiple_of(i * 16, 16)
             w = wcol[pl.ds(at, 16), :]
             w = jnp.concatenate([w, w, w, w], axis=1)
@@ -164,6 +198,17 @@
 
         lax.fori_loop(0, 16, rows_of_table, 0)
 
+    make_table(0)
+    make_table(1)
+    pl.semaphore_wait(near, 4)
+    for i in (2, 6, 1, 7):
+        greet(row_col, on_y(i))
+        greet(row_col, on_z(i))
+    make_table(2)
+    pl.semaphore_wait(row_col, 8)
+    for i in FAR_FIRST:
+        greet(plane, on_z(i))
+
     sub = lax.broadcasted_iota(jnp.int32, (32, 8, 128), 1)
 
     def interleave(p, q):
@@ -173,15 +218,21 @@
         )
 
     def exchange(d, e, h, src, dst):
-        def one(i, carry):
-            k = lax.rem(wave + i, 64)
+        def to(k):
             remote(
                 src.at[e, h, k], dst.at[e, h, wave],
                 wave_ss.at[d, e, h], wave_rs.at[d, e, h], (k, lev),
             )
+
+        def one(n, carry):
+            k = lax.rem(z + 4 + lax.rem(n, 2) * (n + 1) // 2 * 7 + (1 - lax.rem(n, 2)) * n // 2, 8)
+            for i in FAR_FIRST + (0,):
+                to(k * 8 + lax.rem(y + i, 8))
             return carry
 
-        lax.fori_loop(1, 64, one, 0, unroll=7)
+        lax.fori_loop(0, 7, one, 0)
+        for i in FAR_FIRST:
+            to(z * 8 + lax.rem(y + i, 8))
         dst[e, h, wave] = src[e, h, wave]
 
     def exchanged(d, e, h, dst):
@@ -199,13 +250,16 @@
         exchange(0, e, h, a1, c1)
 
     def gather_leg(h):
-        arrived(leg.at[pl.ds(2 * h, 2), pl.ds(0, 7)], leg_rs.at[h])
+        arrived(leg.at[pl.ds(2 * h, 2), pl.ds(0, 4)], leg_ps.at[h])
         for s in (2 * h, 2 * h + 1):
             leg_t[s] = leg[s].reshape(256, 256).T
 
+    relay_leg(0)
+    make_table(3)
     gather_leg(0)
-    pl.semaphore_wait(ready, 7)
+    pl.semaphore_wait(plane, 7)
     legendre(0, 0)
+    relay_leg(1)
     gather_leg(1)
     legendre(0, 1)
     legendre(1, 0)
@@ -217,7 +271,7 @@
     bands = lax.broadcasted_iota(jnp.int32, (8, 64), 0)
     scales = []
     for t in range(4):
-        line = jnp.sum(jnp.where(bands == band_s[t], scale[...], 0.0), axis=0, keepdims=True)
+        line = jnp.sum(jnp.where(bands == band_v[:, t : t + 1], scale[...], 0.0), axis=0, keepdims=True)
         square = jnp.where(diagonal, jnp.broadcast_to(line, (64, 64)), 0.0)
         scales.append(jnp.sum(square, axis=1, keepdims=True))
     first_half = lax.broadcasted_iota(jnp.int32, (256, 128), 1) < 64
@@ -296,8 +350,8 @@
 def shards(control, wave_of_slot, legendre, vertical, points, lat_band, grid_scale, obs_weight):
     members, slots, rows_dev = control.shape[0], control.shape[1], control.shape[2]
     flat = control.reshape(members * slots * rows_dev, 1024)
-    smem = pl.BlockSpec(memory_space=pltpu.SMEM)
     vmem = pl.BlockSpec(memory_space=pltpu.VMEM)
+    hbm = pl.BlockSpec(memory_space=pltpu.HBM)
     wide = (2, 2, 64, 8, 128)
     increment, gradient = pl.pallas_call(
         kernel,
@@ -305,9 +359,12 @@
             jax.ShapeDtypeStruct((2, 4, 64, 512), BF16),
             jax.ShapeDtypeStruct((2, 128, 1024), BF16),
         ),
-        in_specs=[smem] * 3 + [vmem] * 6,
+        in_specs=[hbm] * 3 + [vmem] * 5,
         out_specs=(vmem, vmem),
         scratch_shapes=[
+            pltpu.VMEM((2, 128), jnp.int32),
+            pltpu.VMEM((1, 4), jnp.int32),
+            pltpu.VMEM((1, 4), jnp.int32),
             pltpu.VMEM((4, 128, 128), BF16),
             pltpu.VMEM((16, 256, 256), BF16),
             pltpu.VMEM((8, 2, 4, 32, 128), BF16),
@@ -323,7 +380,11 @@
             pltpu.VMEM(wide, BF16),
             pltpu.VMEM((8, 2, 4, 32, 128), BF16),
             pltpu.VMEM((8, 2, 4, 32, 128), BF16),
+            pltpu.SemaphoreType.DMA((3,)),
             pltpu.SemaphoreType.REGULAR,
+            pltpu.SemaphoreType.REGULAR,
+            pltpu.SemaphoreType.REGULAR,
+            pltpu.SemaphoreType.DMA((2,)),
             pltpu.SemaphoreType.DMA((2,)),
             pltpu.SemaphoreType.DMA((2,)),
             pltpu.SemaphoreType.DMA((2, 2, 2)),
@@ -335,8 +396,7 @@
             collective_id=0, has_side_effects=True, vmem_limit_bytes=24_000_000
         ),
     )(
-        wave_of_slot, points, lat_band, wave_of_slot.reshape(2, 128),
-        flat, legendre, vertical.reshape(16, 128, 128), grid_scale, obs_weight,
+        wave_of_slot.reshape(2, 128), points.reshape(1, 4), lat_band.reshape(1, 4), flat, legendre, vertical.reshape(16, 128, 128), grid_scale, obs_weight,
     )
     return increment, gradient.reshape(control.shape)
 

time: 64 us -> 57.8 us (0.903)
  Pallas kernels: 59.3 us -> 53.1 us
    pallas_call x1, Pallas kernels: 59.3 us -> 53.1 us  [shards(): pl.pallas_call(kernel, out_shape=(jax.ShapeDtypeStruct((2, 4, 64, 512), B...]
where the time goes in v3:
time: 57.8 us; the launch traced here: 57.6 us
  Pallas kernels  53.1 us (92%)
  local copies, waits for them, and re-layouts  3.78 us (7%)
  between operations  0.74 us (1%)
    pallas_call x1, Pallas kernels, shards(): pl.pallas_call(kernel, out_shape=(jax.ShapeDtypeStruct((2, 4, 64, 512), B...  53.1 us
    unnamed x16, local copies, waits for them, and re-layouts  2.61 us
    reshape x1, local copies, waits for them, and re-layouts, shards(): return (increment, gradient.reshape(control.shape))  1.17 us

profile of v3, /device:TPU:1, one launch (start us, length us, event | category | flops | bytes accessed | tf_op | source)
XLA Modules:
  0.0 57.6 jit_solution(11235468826636028399)
XLA Ops:
  0.6 0.0 copy-start
  0.6 0.0 copy-start.1
  0.7 0.0 copy-start.2
  0.7 0.0 copy-start.3
  0.7 0.0 copy-start.6
  0.7 1.2 %copy.10 = bf16[32,8,2,512]{3,1,2,0:T(8,128)(2,1)S(1)} copy(bf16[32,8,2,512]{3,2,1,0:T(2,128)(2,1)} %bitcast.12) | data formatting | bytes 1048576
  1.9 0.0 copy-start.4
  1.9 0.0 copy-start.5
  1.9 0.0 copy-done
  1.9 0.0 copy-done.1
  1.9 0.0 copy-done.2
  1.9 0.0 copy-done.3
  1.9 0.0 copy-done.6
  1.9 0.6 %copy-done.4 = s32[256]{0:T(256)S(1)} copy-done((s32[256]{0:T(256)S(1)}, s32[256]{0:T(256)}, u32[]{:S(2)}) %copy-start.4) | copy-done | bytes 1048
  2.6 0.0 copy-done.5
  2.6 53.1 %shard_map.95 = (bf16[2,4,64,512]{3,2,1,0:T(8,128)(2,1)S(1)}, bf16[2,128,1024]{2,1,0:T(8,128)(2,1)S(1)}) custom-call(s32[2,128]{1,0:T(2,128)S(1)} %bitcast.9, s32[1,4]{1,0:T(1,128)S(1)} %bitcast.10, s32[1,4]{1,0:T(1,128)S(1)} %bitcast.11, bf16[256,1024]{1,0:T(8,128)(2,1)S(1)} %bitcast.7, bf16[4,32,256]{2,1,0:T(8,128)(2,1)S(1)} %copy-done.2, ...), custom_call_target="tpu_custom_call" | custom-call | tf_op jit(solution)/shard_map/pallas_call | solution.py:356
  55.6 1.2 %reshape.27 = bf16[2,4,32,2,512]{4,3,2,1,0:T(2,128)(2,1)} reshape(bf16[2,128,1024]{2,1,0:T(8,128)(2,1)S(1)} %get-tuple-element.5) | data formatting | bytes 1048576 | tf_op jit(solution)/shard_map/reshape | solution.py:401
  56.8 0.8 %copy.12 = bf16[2,4,64,512]{3,2,1,0:T(8,128)(2,1)} copy(bf16[2,4,64,512]{3,2,1,0:T(8,128)(2,1)S(1)} %get-tuple-element.8) | data formatting | bytes 1048576
Async XLA Ops:
  0.6 1.3 %copy-start = (bf16[4,4,128,128]{3,2,1,0:T(8,128)(2,1)S(1)}, bf16[4,4,128,128]{3,2,1,0:T(8,128)(2,1)}, u32[]{:S(2)}) copy-start(bf16[4,4,128,128]{3,2,1,0:T(8,128)(2,1)} %param.11) | copy-start | bytes 1572868
  0.6 1.3 %copy-start.1 = (bf16[4,64,512]{2,1,0:T(8,128)(2,1)S(1)}, bf16[4,64,512]{2,1,0:T(8,128)(2,1)}, u32[]{:S(2)}) copy-start(bf16[4,64,512]{2,1,0:T(8,128)(2,1)} %obs.1) | copy-start | bytes 786436
  0.7 1.3 %copy-start.2 = (bf16[4,32,256]{2,1,0:T(8,128)(2,1)S(1)}, bf16[4,32,256]{2,1,0:T(8,128)(2,1)}, u32[]{:S(2)}) copy-start(bf16[4,32,256]{2,1,0:T(8,128)(2,1)} %own_leg.1) | copy-start | bytes 196612
  0.7 1.3 %copy-start.3 = (f32[8,64]{1,0:T(8,128)S(1)}, f32[8,64]{1,0:T(8,128)}, u32[]{:S(2)}) copy-start(f32[8,64]{1,0:T(8,128)} %scale.1) | copy-start | bytes 6148
  0.7 1.3 %copy-start.6 = (s32[4]{0:T(128)S(1)}, s32[4]{0:T(128)}, u32[]{:S(2)}) copy-start(s32[4]{0:T(128)} %param.13) | copy-start | bytes 52
  1.9 0.7 %copy-start.4 = (s32[256]{0:T(256)S(1)}, s32[256]{0:T(256)}, u32[]{:S(2)}) copy-start(s32[256]{0:T(256)} %param.9) | copy-start | bytes 3076
  1.9 0.7 %copy-start.5 = (s32[4]{0:T(128)S(1)}, s32[4]{0:T(128)}, u32[]{:S(2)}) copy-start(s32[4]{0:T(128)} %param.12) | copy-start | bytes 52

commit v4 on v3

--- a/solution.py
+++ b/solution.py
@@ -33,24 +33,23 @@
 
 
 def kernel(
-    waves_h, points_h, band_h, ctl, own_leg, ver, scale, obs,
+    waves_h, points_h, band_h, ctl_h, leg_h, ver_h, scale_h, obs_h,
     inc, grad,
-    waves_v, points_v, band_v, mask, mix, send_f, recv_f, leg, leg_t, wcol, table,
-    a1, c1, xf, a2, c2, send_b, recv_b,
-    in_sem, near, row_col, plane, leg_ss, leg_rs, leg_ps, lev_ss, lev_rs, wave_ss, wave_rs,
+    waves_v, points_v, band_v, ctl, own_leg, ver, scale, obs, rows, mask, mix, send_f, recv_f, leg, leg_t, wcol, table,
+    a1, c1, part_sum, heavy, xf, a2, c2, send_b, recv_b,
+    in_sem, row_col, plane, leg_ss, leg_rs, leg_ps, lev_ss, lev_rs, wave_ss, wave_rs,
 ):
     wave = lax.axis_index("wave")
     lev = lax.axis_index("lev")
     z = wave // 8
     y = lax.rem(wave, 8)
 
-    small = [
-        pltpu.make_async_copy(src, dst, in_sem.at[i])
-        for i, (src, dst) in enumerate(
-            ((waves_h, waves_v), (points_h, points_v), (band_h, band_v))
-        )
-    ]
-    for copy in small:
+    pairs = (
+        (ver_h, ver), (waves_h, waves_v), (ctl_h, ctl), (leg_h, own_leg),
+        (points_h, points_v), (band_h, band_v), (scale_h, scale), (obs_h, obs),
+    )
+    ins = [pltpu.make_async_copy(src, dst, in_sem.at[i]) for i, (src, dst) in enumerate(pairs)]
+    for copy in ins:
         copy.start()
     barrier = pltpu.get_barrier_semaphore()
 
@@ -68,9 +67,11 @@
 
     for i in FAR_FIRST:
         greet(barrier, (wave, lev_peer(i)))
-    for i in (1, 7):
+    for i in (2, 6, 1, 7):
         greet(barrier, on_y(i))
         greet(barrier, on_z(i))
+
+    ins[0].wait()
 
     def lay(i, carry):
         zero = jnp.zeros((64, 128), BF16)
@@ -85,8 +86,7 @@
 
     lax.fori_loop(0, COV_BANDS * VARIABLES, lay, 0)
 
-    for copy in small:
-        copy.wait()
+    ins[1].wait()
 
     row = lax.broadcasted_iota(jnp.int32, (128, 128), 0)
     slot = row // 32
@@ -101,8 +101,10 @@
         chosen = (total <= WAVES - 1) & (band == b)
         mask[b] = jnp.where(chosen, 1.0, 0.0).astype(BF16)
 
+    ins[2].wait()
+    rows[...] = ctl[...].astype(F32)
     for a in range(VARIABLES):
-        both = [ctl[:, a * 128 : a * 128 + 128], ctl[:, 512 + a * 128 : 640 + a * 128]]
+        both = [rows[pl.ds(2 * a + p, 256, stride=8), :].astype(BF16) for p in range(2)]
         out = jnp.zeros((256, 256), F32)
         for b in range(COV_BANDS):
             m = jnp.concatenate([mask[b], mask[b]], axis=0)
@@ -112,10 +114,11 @@
         for half in range(2):
             send_f[2 * a + half] = out[:, half * 128 : half * 128 + 128].reshape(2, 4, 32, 128)
 
-    pl.semaphore_wait(barrier, 11)
-    for i in (1, 7):
-        greet(near, on_y(i))
-        greet(near, on_z(i))
+    ins[3].wait()
+    pl.semaphore_wait(barrier, 15)
+    for i in (2, 6, 1, 7):
+        greet(row_col, on_y(i))
+        greet(row_col, on_z(i))
 
     def remote(src, dst, ss, rs, who):
         pltpu.make_async_remote_copy(
@@ -192,19 +195,17 @@
             s = x * x
             factor = jnp.where(w == 0.0, 1.0, 2.0) * (1.0 / 32.0)
             factor = jnp.where(j < count, factor, 0.0)
-            table[t, 0, pl.ds(at, 16), :] = (factor * polynomial(COS, s)).astype(BF16)
-            table[t, 1, pl.ds(at, 16), :] = (-factor * (x * polynomial(SIN, s))).astype(BF16)
+            to = pl.multiple_of(lax.rem(i, 8) * 16, 16)
+            table[t, i // 8, 0, pl.ds(to, 16), :] = (factor * polynomial(COS, s)).astype(BF16)
+            table[t, i // 8, 1, pl.ds(to, 16), :] = (-factor * (x * polynomial(SIN, s))).astype(BF16)
             return carry
 
         lax.fori_loop(0, 16, rows_of_table, 0)
 
+    for copy in ins[4:]:
+        copy.wait()
     make_table(0)
     make_table(1)
-    pl.semaphore_wait(near, 4)
-    for i in (2, 6, 1, 7):
-        greet(row_col, on_y(i))
-        greet(row_col, on_z(i))
-    make_table(2)
     pl.semaphore_wait(row_col, 8)
     for i in FAR_FIRST:
         greet(plane, on_z(i))
@@ -254,6 +255,7 @@
         for s in (2 * h, 2 * h + 1):
             leg_t[s] = leg[s].reshape(256, 256).T
 
+    make_table(2)
     relay_leg(0)
     make_table(3)
     gather_leg(0)
@@ -274,37 +276,43 @@
         line = jnp.sum(jnp.where(bands == band_v[:, t : t + 1], scale[...], 0.0), axis=0, keepdims=True)
         square = jnp.where(diagonal, jnp.broadcast_to(line, (64, 64)), 0.0)
         scales.append(jnp.sum(square, axis=1, keepdims=True))
-    first_half = lax.broadcasted_iota(jnp.int32, (256, 128), 1) < 64
+    first_half = lax.broadcasted_iota(jnp.int32, (128, 128), 1) < 64
+
+    def synthesis(h, t):
+        x = xf[h, pl.ds(t, 128, stride=4), :].T.astype(BF16)
+        x = jnp.concatenate([x[0:64], x[64:128]], axis=1)
+        return dot(x, table[t, h].reshape(256, LONGITUDES))
+
+    def analysis(e, h):
+        for t in range(4):
+            out = dot(table[t, h].reshape(256, LONGITUDES), heavy[t], ((1,), (1,)))
+            xf[h, pl.ds(t, 128, stride=4), :] = jnp.where(first_half, out[0:128], out[128:256])
+        a2[e, h] = xf[h].reshape(64, 8, 128).astype(BF16)
+        exchange(1, e, h, a2, c2)
 
     def grid_point(e):
-        for h in range(2):
-            exchanged(0, e, h, c1)
-            xf[h] = c1[e, h].astype(F32).reshape(512, 128)
-        backs = []
+        exchanged(0, e, 0, c1)
+        xf[0] = c1[e, 0].astype(F32).reshape(512, 128)
         for t in range(4):
-            x = jnp.concatenate([xf[h, pl.ds(t, 128, stride=4), :] for h in range(2)], axis=0)
-            xt = x.T.astype(BF16)
-            got = dot(xt[0:64], table[t, 0]) + dot(xt[64:128], table[t, 1])
+            part_sum[t] = synthesis(0, t)
+        exchanged(0, e, 1, c1)
+        xf[1] = c1[e, 1].astype(F32).reshape(512, 128)
+        for t in range(4):
+            got = part_sum[t] + synthesis(1, t)
             made = (got * scales[t]).astype(BF16)
             inc[e, t] = made
-            heavy = (made.astype(F32) * obs[t].astype(F32) * scales[t]).astype(BF16)
-            twice = jnp.concatenate([heavy, heavy], axis=0)
-            real = dot(table[t, 0], twice, ((1,), (1,)))
-            imag = dot(table[t, 1], twice, ((1,), (1,)))
-            backs.append(jnp.where(first_half, real, imag))
-        for t in range(4):
-            for h in range(2):
-                xf[h, pl.ds(t, 128, stride=4), :] = backs[t][h * 128 : h * 128 + 128]
-        for h in range(2):
-            a2[e, h] = xf[h].reshape(64, 8, 128).astype(BF16)
-            exchange(1, e, h, a2, c2)
+            weighted = (made.astype(F32) * obs[t].astype(F32) * scales[t]).astype(BF16)
+            heavy[t, 0:64] = weighted
+            heavy[t, 64:128] = weighted
+        analysis(e, 0)
+        analysis(e, 1)
 
     grid_point(0)
     grid_point(1)
     def legendre_back(e, h):
         exchanged(1, e, h, c2)
-        rows = c2[e, h].astype(F32).reshape(32, 2, 8, 128)
-        for i, piece in enumerate(interleave(rows[:, 0], rows[:, 1])):
+        got = c2[e, h].astype(F32).reshape(32, 2, 8, 128)
+        for i, piece in enumerate(interleave(got[:, 0], got[:, 1])):
             s = 2 * h + i
             out = dot(leg[s].reshape(256, 256), piece.reshape(256, 128).astype(BF16))
             out = out.astype(BF16).reshape(8, 32, 128)
@@ -328,9 +336,9 @@
             for b in range(COV_BANDS):
                 x = jnp.concatenate([part * mask[b] for part in both], axis=1)
                 out = out + dot(x, mix[b * VARIABLES + a])
-            out = out.astype(BF16)
-            grad[e, :, a * 128 : a * 128 + 128] = out[:, 0:128]
-            grad[e, :, 512 + a * 128 : 640 + a * 128] = out[:, 128:256]
+            for p in range(2):
+                rows[pl.ds(1024 * e + 2 * a + p, 128, stride=8), :] = out[:, p * 128 : p * 128 + 128]
+        grad[pl.ds(1024 * e, 1024), :] = rows[pl.ds(1024 * e, 1024), :].astype(BF16)
 
     for h in range(2):
         legendre_back(0, h)
@@ -349,7 +357,8 @@
 
 def shards(control, wave_of_slot, legendre, vertical, points, lat_band, grid_scale, obs_weight):
     members, slots, rows_dev = control.shape[0], control.shape[1], control.shape[2]
-    flat = control.reshape(members * slots * rows_dev, 1024)
+    count = members * slots * rows_dev
+    flat = control.reshape(count, 2, 4, 128).transpose(0, 2, 1, 3).reshape(count * 8, 128)
     vmem = pl.BlockSpec(memory_space=pltpu.VMEM)
     hbm = pl.BlockSpec(memory_space=pltpu.HBM)
     wide = (2, 2, 64, 8, 128)
@@ -357,14 +366,20 @@
         kernel,
         out_shape=(
             jax.ShapeDtypeStruct((2, 4, 64, 512), BF16),
-            jax.ShapeDtypeStruct((2, 128, 1024), BF16),
+            jax.ShapeDtypeStruct((2048, 128), BF16),
         ),
-        in_specs=[hbm] * 3 + [vmem] * 5,
+        in_specs=[hbm] * 8,
         out_specs=(vmem, vmem),
         scratch_shapes=[
             pltpu.VMEM((2, 128), jnp.int32),
             pltpu.VMEM((1, 4), jnp.int32),
             pltpu.VMEM((1, 4), jnp.int32),
+            pltpu.VMEM((2048, 128), BF16),
+            pltpu.VMEM((4, 32, 256), BF16),
+            pltpu.VMEM((16, 128, 128), BF16),
+            pltpu.VMEM((8, 64), F32),
+            pltpu.VMEM((4, 64, 512), BF16),
+            pltpu.VMEM((2048, 128), F32),
             pltpu.VMEM((4, 128, 128), BF16),
             pltpu.VMEM((16, 256, 256), BF16),
             pltpu.VMEM((8, 2, 4, 32, 128), BF16),
@@ -372,16 +387,17 @@
             pltpu.VMEM((4, 8, 32, 256), BF16),
             pltpu.VMEM((4, 256, 256), BF16),
             pltpu.VMEM((256, 128), F32),
-            pltpu.VMEM((4, 2, 256, 512), BF16),
+            pltpu.VMEM((4, 2, 2, 128, 512), BF16),
             pltpu.VMEM(wide, BF16),
             pltpu.VMEM(wide, BF16),
+            pltpu.VMEM((4, 64, 512), F32),
+            pltpu.VMEM((4, 128, 512), BF16),
             pltpu.VMEM((2, 512, 128), F32),
             pltpu.VMEM(wide, BF16),
             pltpu.VMEM(wide, BF16),
             pltpu.VMEM((8, 2, 4, 32, 128), BF16),
             pltpu.VMEM((8, 2, 4, 32, 128), BF16),
-            pltpu.SemaphoreType.DMA((3,)),
-            pltpu.SemaphoreType.REGULAR,
+            pltpu.SemaphoreType.DMA((8,)),
             pltpu.SemaphoreType.REGULAR,
             pltpu.SemaphoreType.REGULAR,
             pltpu.SemaphoreType.DMA((2,)),
@@ -396,8 +412,15 @@
             collective_id=0, has_side_effects=True, vmem_limit_bytes=24_000_000
         ),
     )(
-        wave_of_slot.reshape(2, 128), points.reshape(1, 4), lat_band.reshape(1, 4), flat, legendre, vertical.reshape(16, 128, 128), grid_scale, obs_weight,
+        *(
+            pltpu.with_memory_space_constraint(x, pltpu.HBM)
+            for x in (
+                wave_of_slot.reshape(2, 128), points.reshape(1, 4), lat_band.reshape(1, 4), flat,
+                legendre, vertical.reshape(16, 128, 128), grid_scale, obs_weight,
+            )
+        )
     )
+    gradient = gradient.reshape(count, 4, 2, 128).transpose(0, 2, 1, 3)
     return increment, gradient.reshape(control.shape)
 
 

time: 57.8 us -> 55.3 us (0.957)
  local copies, waits for them, and re-layouts: 3.78 us -> 1.59 us
    reshape x1 -> x0, local copies, waits for them, and re-layouts: 1.17 us -> none  [shards(): return (increment, gradient.reshape(control.shape))]
    unnamed x16 -> x2, local copies, waits for them, and re-layouts: 2.61 us -> 1.59 us
where the time goes in v4:
time: 55.3 us; the launch traced here: 55.2 us
  Pallas kernels  52.9 us (96%)
  local copies, waits for them, and re-layouts  1.59 us (3%)
  between operations  0.64 us (1%)
    pallas_call x1, Pallas kernels, shards(): pl.pallas_call(kernel, out_shape=(jax.ShapeDtypeStruct((2, 4, 64, 512), B...  52.9 us
    unnamed x2, local copies, waits for them, and re-layouts  1.59 us

profile of v4, /device:TPU:1, one launch (start us, length us, event | category | flops | bytes accessed | tf_op | source)
XLA Modules:
  0.0 55.2 jit_solution(9769048664945547577)
XLA Ops:
  0.6 52.9 %shard_map.95 = (bf16[2,4,64,512]{3,2,1,0:T(8,128)(2,1)S(1)}, bf16[2048,128]{1,0:T(8,128)(2,1)S(1)}) custom-call(s32[2,128]{1,0:T(2,128)} %bitcast.17, s32[1,4]{1,0:T(1,128)} %bitcast.18, s32[1,4]{1,0:T(1,128)} %bitcast.19, bf16[2048,128]{1,0:T(8,128)(2,1)} %bitcast.15, bf16[4,32,256]{2,1,0:T(8,128)(2,1)} %leg_h.1, bf16[16,128,128]{2,1,0:T(8,128)(2,1)} %bitcast.16, ...), custom_call_target="tpu_custom_call" | custom-call | tf_op jit(solution)/shard_map/pallas_call | solution.py:365
  53.6 0.8 %copy.14 = bf16[2,4,64,512]{3,2,1,0:T(8,128)(2,1)} copy(bf16[2,4,64,512]{3,2,1,0:T(8,128)(2,1)S(1)} %get-tuple-element.8) | data formatting | bytes 1048576
  54.4 0.8 %copy.15 = bf16[2,4,32,2,512]{4,3,2,1,0:T(2,128)(2,1)} copy(bf16[2,4,32,2,512]{4,3,2,1,0:T(2,128)(2,1)S(1)} %bitcast.14) | data formatting | bytes 1048576

commit v5 on v4

--- a/solution.py
+++ b/solution.py
@@ -44,6 +44,22 @@
     z = wave // 8
     y = lax.rem(wave, 8)
 
+    barrier = pltpu.get_barrier_semaphore()
+
+    def greet(sem, who):
+        pl.semaphore_signal(sem, inc=1, device_id=who, device_id_type=MESH)
+
+    def on_y(i):
+        return (z * 8 + lax.rem(y + i, 8), lev)
+
+    def on_z(i):
+        return (lax.rem(z + i, 8) * 8 + y, lev)
+
+    def lev_peer(i):
+        return lax.rem(lev + i, 8)
+
+    for i in FAR_FIRST:
+        greet(barrier, (wave, lev_peer(i)))
     pairs = (
         (ver_h, ver), (waves_h, waves_v), (ctl_h, ctl), (leg_h, own_leg),
         (points_h, points_v), (band_h, band_v), (scale_h, scale), (obs_h, obs),
@@ -51,40 +67,9 @@
     ins = [pltpu.make_async_copy(src, dst, in_sem.at[i]) for i, (src, dst) in enumerate(pairs)]
     for copy in ins:
         copy.start()
-    barrier = pltpu.get_barrier_semaphore()
-
-    def greet(sem, who):
-        pl.semaphore_signal(sem, inc=1, device_id=who, device_id_type=MESH)
-
-    def on_y(i):
-        return (z * 8 + lax.rem(y + i, 8), lev)
-
-    def on_z(i):
-        return (lax.rem(z + i, 8) * 8 + y, lev)
-
-    def lev_peer(i):
-        return lax.rem(lev + i, 8)
-
-    for i in FAR_FIRST:
-        greet(barrier, (wave, lev_peer(i)))
     for i in (2, 6, 1, 7):
         greet(barrier, on_y(i))
         greet(barrier, on_z(i))
-
-    ins[0].wait()
-
-    def lay(i, carry):
-        zero = jnp.zeros((64, 128), BF16)
-        v = ver[i]
-        for half in range(2):
-            piece = v[half * 64 : half * 64 + 64]
-            mix[i, half * 128 : half * 128 + 64, 0:128] = piece
-            mix[i, half * 128 : half * 128 + 64, 128:256] = zero
-            mix[i, half * 128 + 64 : half * 128 + 128, 0:128] = zero
-            mix[i, half * 128 + 64 : half * 128 + 128, 128:256] = piece
-        return carry
-
-    lax.fori_loop(0, COV_BANDS * VARIABLES, lay, 0)
 
     ins[1].wait()
 
@@ -101,25 +86,6 @@
         chosen = (total <= WAVES - 1) & (band == b)
         mask[b] = jnp.where(chosen, 1.0, 0.0).astype(BF16)
 
-    ins[2].wait()
-    rows[...] = ctl[...].astype(F32)
-    for a in range(VARIABLES):
-        both = [rows[pl.ds(2 * a + p, 256, stride=8), :].astype(BF16) for p in range(2)]
-        out = jnp.zeros((256, 256), F32)
-        for b in range(COV_BANDS):
-            m = jnp.concatenate([mask[b], mask[b]], axis=0)
-            x = jnp.concatenate([part * m for part in both], axis=1)
-            out = out + dot(x, mix[b * VARIABLES + a], ((1,), (1,)))
-        out = out.astype(BF16)
-        for half in range(2):
-            send_f[2 * a + half] = out[:, half * 128 : half * 128 + 128].reshape(2, 4, 32, 128)
-
-    ins[3].wait()
-    pl.semaphore_wait(barrier, 15)
-    for i in (2, 6, 1, 7):
-        greet(row_col, on_y(i))
-        greet(row_col, on_z(i))
-
     def remote(src, dst, ss, rs, who):
         pltpu.make_async_remote_copy(
             src, dst, ss, rs, device_id=who, device_id_type=MESH
@@ -160,10 +126,36 @@
                 lev_ss.at[0, e, h], lev_rs.at[0, e, h], (wave, v),
             )
 
+    lane_low = lax.broadcasted_iota(jnp.int32, (128, 128), 1) < 64
+
+    def vertical(e):
+        for a in range(VARIABLES):
+            x = [rows[pl.ds(1024 * e + 2 * a + p, 128, stride=8), :].astype(BF16) for p in range(2)]
+            x = [jnp.concatenate([part * mask[b] for b in range(COV_BANDS)], axis=1) for part in x]
+            matrices = [ver[b * VARIABLES + a] for b in range(COV_BANDS)]
+            out = dot(
+                jnp.concatenate(x, axis=0), jnp.concatenate(matrices, axis=1), ((1,), (1,))
+            )
+            real, imag = out[0:128], out[128:256]
+            low = jnp.where(lane_low, real, pltpu.roll(imag, 64, 1))
+            high = jnp.where(lane_low, pltpu.roll(real, 64, 1), imag)
+            send_f[2 * a, e] = low.astype(BF16).reshape(4, 32, 128)
+            send_f[2 * a + 1, e] = high.astype(BF16).reshape(4, 32, 128)
+
+    ins[2].wait()
+    rows[...] = ctl[...].astype(F32)
+    ins[0].wait()
+    vertical(0)
+    ins[3].wait()
+    pl.semaphore_wait(barrier, 15)
+    for i in (2, 6, 1, 7):
+        greet(row_col, on_y(i))
+        greet(row_col, on_z(i))
     send_leg(0)
     send_spec(0, 0)
     send_leg(1)
     send_spec(0, 1)
+    vertical(1)
     send_spec(1, 0)
     send_spec(1, 1)
     for s in range(4):
@@ -201,6 +193,19 @@
             return carry
 
         lax.fori_loop(0, 16, rows_of_table, 0)
+
+    def lay(i, carry):
+        zero = jnp.zeros((64, 128), BF16)
+        v = ver[i]
+        for half in range(2):
+            piece = v[half * 64 : half * 64 + 64]
+            mix[i, half * 128 : half * 128 + 64, 0:128] = piece
+            mix[i, half * 128 : half * 128 + 64, 128:256] = zero
+            mix[i, half * 128 + 64 : half * 128 + 128, 0:128] = zero
+            mix[i, half * 128 + 64 : half * 128 + 128, 128:256] = piece
+        return carry
+
+    lax.fori_loop(0, COV_BANDS * VARIABLES, lay, 0)
 
     for copy in ins[4:]:
         copy.wait()
@@ -353,6 +358,17 @@
             for d in range(2):
                 arrived(recv_f.at[e, pl.ds(2 * h, 2), pl.ds(0, 7)], lev_ss.at[d, e, h])
                 arrived(c1.at[e, h, pl.ds(0, 63)], wave_ss.at[d, e, h])
+
+
+def deliver(inc, grad, inc_h, grad_h, sem):
+    copies = (
+        pltpu.make_async_copy(inc, inc_h, sem.at[0]),
+        pltpu.make_async_copy(grad, grad_h, sem.at[1]),
+    )
+    for copy in copies:
+        copy.start()
+    for copy in copies:
+        copy.wait()
 
 
 def shards(control, wave_of_slot, legendre, vertical, points, lat_band, grid_scale, obs_weight):
@@ -420,6 +436,17 @@
             )
         )
     )
+    increment, gradient = pl.pallas_call(
+        deliver,
+        out_shape=(
+            jax.ShapeDtypeStruct((2, 4, 64, 512), BF16),
+            jax.ShapeDtypeStruct((2048, 128), BF16),
+        ),
+        in_specs=[vmem, vmem],
+        out_specs=(hbm, hbm),
+        scratch_shapes=[pltpu.SemaphoreType.DMA((2,))],
+        compiler_params=pltpu.CompilerParams(vmem_limit_bytes=24_000_000),
+    )(increment, gradient)
     gradient = gradient.reshape(count, 4, 2, 128).transpose(0, 2, 1, 3)
     return increment, gradient.reshape(control.shape)
 

time: 55.3 us -> 54.3 us (0.982)
  local copies, waits for them, and re-layouts: 1.59 us -> 0 us
  Pallas kernels: 52.9 us -> 53.5 us
    unnamed x2 -> x0, local copies, waits for them, and re-layouts: 1.59 us -> none
    pallas_call x0 -> x1, Pallas kernels: none -> 0.99 us  [shards(): pl.pallas_call(deliver, out_shape=(jax.ShapeDtypeStruct((2, 4, 64, 512),...]
where the time goes in v5:
time: 54.3 us; the launch traced here: 54.1 us
  Pallas kernels  53.5 us (99%)
  between operations  0.64 us (1%)
    pallas_call x1, Pallas kernels, shards(): pl.pallas_call(kernel, out_shape=(jax.ShapeDtypeStruct((2, 4, 64, 512), B...  52.5 us

profile of v5, /device:TPU:1, one launch (start us, length us, event | category | flops | bytes accessed | tf_op | source)
XLA Modules:
  0.0 54.1 jit_solution(6851336248557511204)
XLA Ops:
  0.6 52.5 %shard_map.95 = (bf16[2,4,64,512]{3,2,1,0:T(8,128)(2,1)S(1)}, bf16[2048,128]{1,0:T(8,128)(2,1)S(1)}) custom-call(s32[2,128]{1,0:T(2,128)} %bitcast.16, s32[1,4]{1,0:T(1,128)} %bitcast.17, s32[1,4]{1,0:T(1,128)} %bitcast.18, bf16[2048,128]{1,0:T(8,128)(2,1)} %bitcast.14, bf16[4,32,256]{2,1,0:T(8,128)(2,1)} %leg_h.1, bf16[16,128,128]{2,1,0:T(8,128)(2,1)} %bitcast.15, ...), custom_call_target="tpu_custom_call" | custom-call | tf_op jit(solution)/shard_map/pallas_call | solution.py:381
  53.1 1.0 %shard_map.96 = (bf16[2,4,64,512]{3,2,1,0:T(8,128)(2,1)}, bf16[2048,128]{1,0:T(8,128)(2,1)}) custom-call(bf16[2,4,64,512]{3,2,1,0:T(8,128)(2,1)S(1)} %get-tuple-element.6.inc, bf16[2048,128]{1,0:T(8,128)(2,1)S(1)} %get-tuple-element.7.grad), custom_call_target="tpu_custom_call" | custom-call | tf_op jit(solution)/shard_map/pallas_call | solution.py:439

commit v6 on v5

--- a/solution.py
+++ b/solution.py
@@ -15,6 +15,10 @@
 F32 = jnp.float32
 BF16 = jnp.bfloat16
 FAR_FIRST = (4, 3, 5, 2, 6, 1, 7)
+BY_DISTANCE = sorted(
+    ((i, j) for i in range(8) for j in range(8) if i + j > 0),
+    key=lambda at: -min(at[0], 8 - at[0]) - min(at[1], 8 - at[1]),
+)
 SIN = (6.283185302498671, -41.34170040100665, 81.6051311559332, -76.70301094142194,
        42.02588917305049, -14.899698808670236, 3.237922486217859)
 COS = (0.9999999998851921, -19.739208743292323, 64.93938906426658, -85.45665800487392,
@@ -230,15 +234,8 @@
                 wave_ss.at[d, e, h], wave_rs.at[d, e, h], (k, lev),
             )
 
-        def one(n, carry):
-            k = lax.rem(z + 4 + lax.rem(n, 2) * (n + 1) // 2 * 7 + (1 - lax.rem(n, 2)) * n // 2, 8)
-            for i in FAR_FIRST + (0,):
-                to(k * 8 + lax.rem(y + i, 8))
-            return carry
-
-        lax.fori_loop(0, 7, one, 0)
-        for i in FAR_FIRST:
-            to(z * 8 + lax.rem(y + i, 8))
+        for i, j in BY_DISTANCE:
+            to(lax.rem(z + i, 8) * 8 + lax.rem(y + j, 8))
         dst[e, h, wave] = src[e, h, wave]
 
     def exchanged(d, e, h, dst):

time: 54.3 us -> 53.6 us (0.987)
  Pallas kernels: 53.5 us -> 52.8 us
    pallas_call x1, Pallas kernels: 52.5 us -> 51.9 us  [shards(): pl.pallas_call(kernel, out_shape=(jax.ShapeDtypeStruct((2, 4, 64, 512), B...]
where the time goes in v6:
time: 53.6 us; the launch traced here: 53.5 us
  Pallas kernels  52.8 us (99%)
  between operations  0.64 us (1%)
    pallas_call x1, Pallas kernels, shards(): pl.pallas_call(kernel, out_shape=(jax.ShapeDtypeStruct((2, 4, 64, 512), B...  51.9 us

profile of v6, /device:TPU:1, one launch (start us, length us, event | category | flops | bytes accessed | tf_op | source)
XLA Modules:
  0.0 53.5 jit_solution(7217650114953442754)
XLA Ops:
  0.6 51.9 %shard_map.95 = (bf16[2,4,64,512]{3,2,1,0:T(8,128)(2,1)S(1)}, bf16[2048,128]{1,0:T(8,128)(2,1)S(1)}) custom-call(s32[2,128]{1,0:T(2,128)} %bitcast.16, s32[1,4]{1,0:T(1,128)} %bitcast.17, s32[1,4]{1,0:T(1,128)} %bitcast.18, bf16[2048,128]{1,0:T(8,128)(2,1)} %bitcast.14, bf16[4,32,256]{2,1,0:T(8,128)(2,1)} %leg_h.1, bf16[16,128,128]{2,1,0:T(8,128)(2,1)} %bitcast.15, ...), custom_call_target="tpu_custom_call" | custom-call | tf_op jit(solution)/shard_map/pallas_call | solution.py:378
  52.5 1.0 %shard_map.96 = (bf16[2,4,64,512]{3,2,1,0:T(8,128)(2,1)}, bf16[2048,128]{1,0:T(8,128)(2,1)}) custom-call(bf16[2,4,64,512]{3,2,1,0:T(8,128)(2,1)S(1)} %get-tuple-element.6.inc, bf16[2048,128]{1,0:T(8,128)(2,1)S(1)} %get-tuple-element.7.grad), custom_call_target="tpu_custom_call" | custom-call | tf_op jit(solution)/shard_map/pallas_call | solution.py:436
